TPU v7x, 128 devices: a whole 4x4x4 slice. The times are simulated.
128 devices in a mesh: cuts: 32 (over x_hi, y, z), event: 4 (over x_lo, core).
Axes of the slice: x: 4 (x_hi: 2, x_lo: 2; x = x_hi * 2 + x_lo), y: 4, z: 4, core: 2. Of those that a mesh axis runs over, the one named last changes fastest.
Arguments:
- kernels: float32 [4, 256, 128, 256], P('event', 'cuts'), may hold values from -24 to 24
- steps: float32 [8, 256, 128, 256], P(None, 'cuts', 'event'), may hold values from -11 to 11
- curvature: float32 [8, 256, 128, 256], P(None, 'cuts', 'event'), may hold values from 0.2 to 5
Outputs:
- gradient: float32 [256, 128, 256], P('cuts', 'event')
- direction: float32 [256, 128, 256], P('cuts', 'event')
All inputs are finite; a program needn't handle non-finite values.
Results may differ from a plain program's by a relative error of at most 0.00021.
Values sent between devices are 32-bit elements; how exact they have to be, the bound alone decides.
No kernel may reach another device: no remote copies, remote signals or barrier semaphores. Data moves between devices by JAX's collectives and lax.ppermute only.
A program may use at most 64 MiB of HBM per device.

v0:
```python
import functools
import math

import jax
import jax.numpy as jnp
from jax import lax
from jax.experimental import pallas as pl
from jax.experimental.pallas import tpu as pltpu
from jax.sharding import Mesh
from jax.sharding import PartitionSpec as P

PAIRS = 8
RIM = 4
CUTS = ("cuts_0", "cuts_1", "cuts_2")
EVENT = ("event_0", "event_1")
CUTS_EVENT = ("cuts_0", "cuts_1", "cuts_2", "event_0", "event_1")
LANES = 128
SQUARES, STEPS_GRADIENT, CHANGES_GRADIENT = 64, 100, 108


def cycle_weights():
    unscaled = [math.exp(-((column - RIM) ** 2) / 4.5) for column in range(2 * RIM + 1)]
    whole = sum(unscaled)
    return [weight / whole for weight in unscaled]


def split(x):
    high = x.astype(jnp.bfloat16)
    low = (x - high.astype(jnp.float32)).astype(jnp.bfloat16)
    return high, low


def dot(a, b):
    return jnp.dot(a, b, preferred_element_type=jnp.float32)


def call(kernel, outs, flops, moved, limit=16, **options):
    return pl.pallas_call(
        kernel,
        out_shape=[jax.ShapeDtypeStruct(*out) for out in outs],
        compiler_params=pltpu.CompilerParams(vmem_limit_bytes=limit << 20),
        cost_estimate=pl.CostEstimate(flops=flops, bytes_accessed=moved, transcendentals=0),
        **options,
    )


def gauss_rows(length, sigma, rows, axis):
    offset = (rows - lax.broadcasted_iota(jnp.int32, rows.shape, axis)).astype(jnp.float32)
    matrix = jnp.exp(-offset * offset / (2.0 * sigma * sigma))
    return matrix / jnp.sum(matrix, axis=axis, keepdims=True)


def gauss_rows(length, sigma, rows, axis):
    offset = (rows - lax.broadcasted_iota(jnp.int32, rows.shape, axis)).astype(jnp.float32)
    matrix = jnp.exp(-offset * offset / (2.0 * sigma * sigma))
    return matrix / jnp.sum(matrix, axis=axis, keepdims=True)


def radial_products(field_ref, weights, keep_ref, pass_ref, send_keep_ref, send_pass_ref):
    for a in range(field_ref.shape[0]):
        both = dot(weights, jnp.concatenate(split(field_ref[a]), axis=0))
        length = both.shape[0] // 2
        rows = length // 4
        out = both[:length] + both[length:]
        for k, ref in enumerate((keep_ref, pass_ref, send_keep_ref, send_pass_ref)):
            ref[a] = out[k * rows : (k + 1) * rows]


def far_radial_kernel(
    kernels_ref, keep_ref, pass_ref, send_keep_ref, send_pass_ref, near_ref, weights_ref, far_ref, semaphores
):
    length = kernels_ref.shape[2]
    odd = lax.rem(cut_number(), 2)
    copies = []
    for piece, ref in enumerate((far_ref, near_ref)):
        source = kernels_ref.at[0, pl.ds(RIM * (odd ^ piece), RIM)]
        copies.append(pltpu.make_async_copy(source, ref, semaphores.at[piece]))
        copies[piece].start()
    part = 2 * lax.axis_index("event_0") + lax.axis_index("event_1")
    rows = length // 4
    local = lax.broadcasted_iota(jnp.int32, (rows, length), 0)

    def weights_of(first):
        order = [first, first ^ 2, first ^ 1, first ^ 3]
        matrix = jnp.concatenate(
            [gauss_rows(length, 3.0, local + rows * block, 1) for block in order], axis=0
        )
        return jnp.concatenate([jnp.concatenate([m, m], axis=1) for m in split(matrix)], axis=0)

    cut = cut_number()
    at_wrap = jnp.logical_or(cut == 0, cut == lax.axis_size(CUTS) - 1)
    weights = weights_of(jnp.where(at_wrap, part ^ 2, part))
    weights_ref[...] = weights_of(part)
    copies[0].wait()
    radial_products(far_ref, weights, keep_ref, pass_ref, send_keep_ref, send_pass_ref)
    copies[1].wait()


def near_radial_kernel(
    near_ref, weights_ref, far_send_keep_ref, keep_ref, pass_ref, rest_ref, high_ref, low_ref
):
    rest_ref[2] = far_send_keep_ref[...]
    parts = (keep_ref, pass_ref, rest_ref.at[1], rest_ref.at[0])
    radial_products(near_ref, weights_ref[...], *parts)
    lats = high_ref.shape[0]
    column = lax.broadcasted_iota(jnp.int32, (lats, lats), 1)
    high_ref[...], low_ref[...] = split(gauss_rows(lats, 4.0, column, 0))


def smoothed(field, high, low):
    count = field.shape[0]
    both = jnp.concatenate(split(field), axis=0)
    out = dot(both, high) + dot(both, low)
    return out[:count] + out[count:]


def latitude_kernel(slot, keep_ref, rest_ref, chip_ref, high_ref, low_ref, plane_ref):
    lons, rows, lats = plane_ref.shape
    summed = (keep_ref[...] + rest_ref[slot] + chip_ref[...]).reshape(lons * rows, lats)
    plane_ref[...] = smoothed(summed, high_ref[...], low_ref[...]).reshape(lons, rows, lats)


def lane_numbers():
    return lax.broadcasted_iota(jnp.int32, (8, LANES), 1)


def tiles(shape):
    return [
        (a, slice(8 * r, 8 * r + 8), slice(LANES * b, LANES * (b + 1)))
        for r in range(shape[1] // 8)
        for b in range(shape[2] // LANES)
        for a in range(shape[0])
    ]


def placed(sums):
    lanes = lane_numbers()
    row = jnp.zeros((8, LANES), jnp.float32)
    for lane, value in sums:
        row = row + jnp.where(lanes == lane, jnp.sum(value, axis=1, keepdims=True), 0.0)
    return row


def spots(shape):
    return [
        (slice(8 * r, 8 * r + 8), slice(LANES * b, LANES * (b + 1)))
        for r in range(shape[0] // 8)
        for b in range(shape[1] // LANES)
    ]


def summed_over(lons, step, size):
    return lax.fori_loop(0, lons, step, [jnp.zeros((8, LANES), jnp.float32)] * size)


def fetch_kernel(curvature_hbm, curvature_ref, semaphore):
    copy = pltpu.make_async_copy(curvature_hbm, curvature_ref, semaphore)
    copy.start()
    copy.wait()


def gram_kernel(steps_ref, curvature_ref, changes_ref, row_ref):
    lons, *plane = steps_ref.shape[1:]
    half = PAIRS // 2
    upper = [(i, j) for i in range(PAIRS) for j in range(i, PAIRS)]

    def first(a, sums):
        for at in spots(plane):
            steps = [steps_ref[(i, a, *at)] for i in range(half)]
            changes = [None] * PAIRS
            for i in range(PAIRS):
                value = steps[i] if i < half else steps_ref[(i, a, *at)]
                changes[i] = curvature_ref[(i, a, *at)] * value
                changes_ref[(i, a, *at)] = changes[i]
            sums = [sums[k] + steps[k // PAIRS] * changes[k % PAIRS] for k in range(half * PAIRS)]
        return sums

    def second(a, sums):
        for at in spots(plane):
            steps = [steps_ref[(i, a, *at)] for i in range(half, PAIRS)]
            changes = [changes_ref[(i, a, *at)] for i in range(PAIRS)]
            sums = [sums[k] + steps[k // PAIRS] * changes[k % PAIRS] for k in range(half * PAIRS)]
        return sums

    def squares(a, sums):
        for at in spots(plane):
            changes = [changes_ref[(i, a, *at)] for i in range(PAIRS)]
            sums = [value + changes[i] * changes[j] for value, (i, j) in zip(sums, upper)]
        return sums

    row = placed(enumerate(summed_over(lons, first, half * PAIRS)))
    row = row + placed(enumerate(summed_over(lons, second, half * PAIRS), half * PAIRS))
    row_ref[...] = row + placed(enumerate(summed_over(lons, squares, len(upper)), SQUARES))


def near_base():
    return RIM * (1 - lax.rem(cut_number(), 2))


def side_products(base, halo_ref, side_ref, inner_ref, steps_ref, changes_ref, gradient_ref, padded_ref):
    lons, rows, lats = gradient_ref.shape
    weights = cycle_weights()
    outer = 2 * base // RIM
    padded_ref[outer] = halo_ref[...]
    padded_ref[1] = side_ref[...]
    padded_ref[2 - outer] = inner_ref[...]
    sums = [jnp.zeros((8, LANES), jnp.float32) for _ in range(2 * PAIRS)]
    for at in spots((rows, lats)):
        padded = [padded_ref[(k, a, *at)] for k in range(3) for a in range(RIM)]
        for a in range(lons):
            value = weights[RIM] * padded[a + RIM]
            for k in range(RIM):
                value = value + weights[k] * (padded[a + k] + padded[a + 2 * RIM - k])
            gradient_ref[(a, *at)] = value
            for pair in range(PAIRS):
                sums[pair] = sums[pair] + steps_ref[(pair, base + a, *at)] * value
                sums[PAIRS + pair] = sums[PAIRS + pair] + changes_ref[(pair, base + a, *at)] * value
    return placed(enumerate(sums, STEPS_GRADIENT))


def near_product_kernel(
    halo_ref, near_ref, far_ref, steps_ref, changes_ref, gram_ref, gradient_ref, row_ref, padded_ref
):
    operands = (halo_ref, near_ref, far_ref, steps_ref, changes_ref, gradient_ref, padded_ref)
    row_ref[...] = gram_ref[...] + side_products(near_base(), *operands)


def far_product_kernel(
    halo_ref, far_ref, near_ref, steps_ref, changes_ref, near_row_ref, gradient_ref, rows_ref, padded_ref
):
    operands = (halo_ref, far_ref, near_ref, steps_ref, changes_ref, gradient_ref, padded_ref)
    row = near_row_ref[...] + side_products(RIM - near_base(), *operands)
    row = jnp.sum(row, axis=0, keepdims=True)
    rows_ref[...] = jnp.broadcast_to(row[None], rows_ref.shape)


def direction_kernel(
    rows_ref, far_ref, near_ref, steps_ref, changes_ref,
    gradient_out, direction_out, direction_ref, semaphores,
):
    sides = ((RIM - near_base(), far_ref), (near_base(), near_ref))
    written = [
        pltpu.make_async_copy(ref, gradient_out.at[pl.ds(base, RIM)], semaphores.at[k])
        for k, (base, ref) in enumerate(sides)
    ]
    for copy in written:
        copy.start()
    row = jnp.broadcast_to(jnp.sum(rows_ref[...], axis=0), (8, LANES))
    lanes = lane_numbers()
    pairs = lax.broadcasted_iota(jnp.int32, (8, LANES), 0)

    def column(lane_of):
        picked = jnp.where(lanes == lane_of, row, 0.0)
        return jnp.broadcast_to(jnp.sum(picked, axis=1, keepdims=True), (8, LANES))

    def element(vector, i):
        return jnp.broadcast_to(vector[i : i + 1], (8, LANES))

    def square_lanes(j):
        low, high = jnp.minimum(pairs, j), jnp.maximum(pairs, j)
        return SQUARES + low * PAIRS - ((low * (low - 1)) >> 1) + high - low

    by_change = [column(pairs * PAIRS + i) for i in range(PAIRS)]
    by_step = [column(pairs + PAIRS * i) for i in range(PAIRS)]
    squares = [column(square_lanes(i)) for i in range(PAIRS)]
    curvs = column(pairs * (PAIRS + 1))
    steps_part = column(pairs + STEPS_GRADIENT)
    changes_part = column(pairs + CHANGES_GRADIENT)
    inverse = 1.0 / curvs
    scaling = element(curvs, PAIRS - 1) / element(squares[PAIRS - 1], PAIRS - 1)
    alphas = [None] * PAIRS
    for i in reversed(range(PAIRS)):
        alphas[i] = element(inverse * steps_part, i)
        steps_part = steps_part - alphas[i] * by_change[i]
        changes_part = changes_part - alphas[i] * squares[i]
    changes_part = scaling * changes_part
    weights = [None] * PAIRS
    for i in range(PAIRS):
        weights[i] = alphas[i] - element(inverse * changes_part, i)
        changes_part = changes_part + weights[i] * by_step[i]
    change_weights = [scaling * alpha for alpha in alphas]
    copies = []
    half = RIM // 2
    for piece in range(4):
        base, gradient_ref = sides[piece // 2]
        first = piece % 2 * half
        for a, r, b in tiles((half, *far_ref.shape[1:])):
            lon = base + first + a
            value = -(scaling * gradient_ref[first + a, r, b])
            for i in range(PAIRS):
                value = value + change_weights[i] * changes_ref[i, lon, r, b]
                value = value - weights[i] * steps_ref[i, lon, r, b]
            direction_ref[half * piece + a, r, b] = value
        if copies:
            copies[-1].start()
        copies.append(
            pltpu.make_async_copy(
                direction_ref.at[pl.ds(half * piece, half)],
                direction_out.at[pl.ds(base + first, half)],
                semaphores.at[2 + piece],
            )
        )
    copies[-1].start()
    for copy in copies + written:
        copy.wait()


def in_hbm(x):
    return pltpu.with_memory_space_constraint(x, pltpu.HBM)


def swapped(x, axis):
    return lax.ppermute(x, axis, [(0, 1), (1, 0)])


def cut_number():
    number = 0
    for axis in CUTS:
        number = number * lax.axis_size(axis) + lax.axis_index(axis)
    return number


def shards(kernels, steps, curvature):
    _, lons, rad_len, lats = kernels.shape
    rows = rad_len // 4
    block = ((lons, rows, lats), jnp.float32)
    size = lons * rows * lats
    half = ((RIM, rows, lats), jnp.float32)
    cuts, events = lax.axis_size(CUTS), lax.axis_size(EVENT)
    table = ((2 * rad_len, 2 * rad_len), jnp.bfloat16)
    flops = 4 * rad_len * kernels.size
    far_keep, far_pass, far_send_keep, far_send_pass, near_field, weights = call(
        far_radial_kernel,
        [half] * 4 + [((RIM, rad_len, lats), jnp.float32), table],
        flops,
        8 * kernels.size,
        in_specs=[pl.BlockSpec(memory_space=pltpu.HBM)],
        scratch_shapes=[
            pltpu.VMEM((RIM, rad_len, lats), jnp.float32),
            pltpu.SemaphoreType.DMA((2,)),
        ],
    )(in_hbm(kernels))
    far_core_pass = swapped(far_send_pass, "event_1")
    square = ((lats, lats), jnp.bfloat16)
    near_keep, near_pass, rest, high, low = call(
        near_radial_kernel,
        [half, half, ((3, RIM, rows, lats), jnp.float32), square, square],
        flops,
        4 * kernels.size,
    )(near_field, weights, far_send_keep)
    far_chip = swapped(far_pass + far_core_pass, "event_0")
    rest = swapped(rest, "event_1")
    near_chip = swapped(near_pass + rest[0], "event_0")
    row = ((8, LANES), jnp.float32)
    (held_curvature,) = call(
        fetch_kernel,
        [(curvature.shape, jnp.float32)],
        0,
        8 * curvature.size,
        in_specs=[pl.BlockSpec(memory_space=pltpu.HBM)],
        scratch_shapes=[pltpu.SemaphoreType.DMA],
    )(in_hbm(curvature))
    changes, gram = call(
        gram_kernel,
        [(steps.shape, jnp.float32), row],
        2 * 108 * size,
        12 * steps.size,
    )(steps, held_curvature)

    def plane_of(slot, *parts):
        kernel = functools.partial(latitude_kernel, slot)
        return call(kernel, [half], 4 * lats * size, 8 * size)(*parts, high, low)[0]

    far_plane = plane_of(2, far_keep, rest, far_chip)
    pairs, returns = [], []
    for c in range(cuts):
        other, flip = (((c - 1) ^ 1) + 1) % cuts, 0
        if c in (0, cuts - 1):
            other, flip = cuts - 1 - c, 2
        for e in range(events):
            pairs.append((c * events + e, other * events + (e ^ flip)))
            returns.append((c * events + e, c * events + (e ^ flip)))
    far_halo = lax.ppermute(far_plane, CUTS_EVENT, pairs)
    far_plane = lax.ppermute(far_plane, CUTS_EVENT, returns)
    near_plane = plane_of(1, near_keep, rest, near_chip)
    near_halo = lax.ppermute(near_plane, CUTS, [(c, c ^ 1) for c in range(cuts)])
    padded = [pltpu.VMEM((3, RIM, rows, lats), jnp.float32)]
    near_gradient, near_row = call(
        near_product_kernel, [half, row], 2 * 20 * size, 4 * 10 * size, scratch_shapes=padded
    )(near_halo, near_plane, far_plane, steps, changes, gram)
    far_gradient, outgoing = call(
        far_product_kernel,
        [half, ((cuts * events, 1, LANES), jnp.float32)],
        2 * 20 * size,
        4 * 10 * size,
        scratch_shapes=padded,
    )(far_halo, far_plane, near_plane, steps, changes, near_row)
    arrived = lax.all_to_all(outgoing, CUTS_EVENT, 0, 0, tiled=True)
    return call(
        direction_kernel,
        [block] * 2,
        2 * 17 * size,
        4 * 18 * size,
        out_specs=[pl.BlockSpec(memory_space=pltpu.HBM)] * 2,
        scratch_shapes=[pltpu.VMEM((lons, rows, lats), jnp.float32), pltpu.SemaphoreType.DMA((6,))],
    )(arrived, far_gradient, near_gradient, steps, changes)


def solution(mesh):
    torus = Mesh(
        mesh.devices.reshape(2, 4, 4, 2, 2), ("cuts_0", "cuts_1", "cuts_2", "event_0", "event_1")
    )
    in_specs = (P(EVENT, CUTS, None, None), P(None, CUTS, EVENT, None), P(None, CUTS, EVENT, None))
    out_specs = (P(CUTS, EVENT, None), P(CUTS, EVENT, None))
    return jax.shard_map(
        shards, mesh=torus, in_specs=in_specs, out_specs=out_specs, check_vma=False
    )
```

profile of v0, /device:TPU:1, one launch (start us, length us, event | category | flops | bytes accessed | tf_op | source)
XLA Modules:
  0.0 46.8 jit_solution(6718913395866439889)
XLA Ops:
  0.6 1.4 %shard_map.50 = (f32[4,32,256]{2,1,0:T(8,128)S(1)}, f32[4,32,256]{2,1,0:T(8,128)S(1)}, f32[4,32,256]{2,1,0:T(8,128)S(1)}, f32[4,32,256]{2,1,0:T(8,128)S(1)}, f32...) custom-call(f32[1,8,128,256]{3,2,1,0:T(8,128)} %kernels_ref.1), custom_call_target="tpu_custom_call" | custom-call | flops 134217728 | bytes 2097152 | tf_op jit(solution)/shard_map/pallas_call | solution.py:332
  2.0 0.4 shard_map.51
  2.4 1.5 %collective-permute-start = (f32[3,4,32,256]{3,2,1,0:T(8,128)S(1)}, f32[3,4,32,256]{3,2,1,0:T(8,128)S(1)}, u32[]{:S(2)}, u32[]{:S(2)}) collective-permute-start(f32[3,4,32,256]{3,2,1,0:T(8,128)S(1)} %get-tuple-element.23), channel_id=1, source_target_pairs={{0,1},{1,0},{2,3},{3,2},{4,5},{5,4},{6,7},{7,6},{8,9},{9,8},{10,11... | collective-permute-start | bytes 1179656 | tf_op jit(solution)/shard_map/ppermute | solution.py:313
  3.9 0.1 collective-permute-start.1
  3.9 1.4 %collective-permute-done.1 = f32[4,32,256]{2,1,0:T(8,128)S(1)} collective-permute-done((f32[4,32,256]{2,1,0:T(8,128)S(1)}, f32[4,32,256]{2,1,0:T(8,128)S(1)}, u32[]{:S(2)}, u32[]{:S(2)}) %collective-permute-start.1) | collective-permute-done | bytes 131104 | tf_op jit(solution)/shard_map/ppermute | solution.py:313
  5.4 1.4 %collective-permute-start.2 = (f32[4,32,256]{2,1,0:T(8,128)S(1)}, f32[4,32,256]{2,1,0:T(8,128)S(1)}, u32[]{:S(2)}, u32[]{:S(2)}) collective-permute-start(f32[4,32,256]{2,1,0:T(8,128)S(1)} %add.6), channel_id=1, source_target_pairs={{0,2},{2,0},{1,3},{3,1},{4,6},{6,4},{5,7},{7,5},{8,10},{10,8},{9,1... | collective-permute-start | bytes 393224 | tf_op jit(solution)/shard_map/ppermute | solution.py:313
  6.8 0.0 collective-permute-done.rest_ref
  6.8 0.2 collective-permute-start.5
  7.1 3.1 %collective-permute-done.2.chip_ref = f32[4,32,256]{2,1,0:T(8,128)S(1)} collective-permute-done((f32[4,32,256]{2,1,0:T(8,128)S(1)}, f32[4,32,256]{2,1,0:T(8,128)S(1)}, u32[]{:S(2)}, u32[]{:S(2)}) %collective-permute-start.2) | collective-permute-done | bytes 131104 | tf_op jit(solution)/shard_map/ppermute | solution.py:313
  10.2 0.2 shard_map.52
  10.4 3.2 %collective-permute-start.4 = (f32[4,32,256]{2,1,0:T(8,128)S(1)}, f32[4,32,256]{2,1,0:T(8,128)S(1)}, u32[]{:S(2)}, u32[]{:S(2)}) collective-permute-start(f32[4,32,256]{2,1,0:T(8,128)S(1)} %shard_map.52), channel_id=1, source_target_pairs={{0,2},{1,3},{2,0},{3,1},{4,4},{5,5},{6,6},{7,7},{8,8},{9,9},{10,10... | collective-permute-start | bytes 393224 | tf_op jit(solution)/shard_map/ppermute | solution.py:384
  13.6 0.0 collective-permute-done.5.chip_ref
  13.7 0.2 shard_map.53.near_ref
  13.9 0.0 copy-start
  13.9 1.2 %collective-permute-start.6 = (f32[4,32,256]{2,1,0:T(8,128)S(1)}, f32[4,32,256]{2,1,0:T(8,128)S(1)}, u32[]{:S(2)}, u32[]{:S(2)}) collective-permute-start(f32[4,32,256]{2,1,0:T(8,128)S(1)} %shard_map.53.near_ref), channel_id=1, source_target_pairs={{0,4},{4,0},{8,12},{12,8},{16,20},{20,16},{24,28},{28,24},{32,36},... | collective-permute-start | bytes 393224 | tf_op jit(solution)/shard_map/ppermute | solution.py:386
  15.1 6.9 %collective-permute-start.3 = (f32[4,32,256]{2,1,0:T(8,128)S(1)}, f32[4,32,256]{2,1,0:T(8,128)S(1)}, u32[]{:S(2)}, u32[]{:S(2)}) collective-permute-start(f32[4,32,256]{2,1,0:T(8,128)S(1)} %shard_map.52), channel_id=1, source_target_pairs={{0,126},{1,127},{2,124},{3,125},{4,8},{5,9},{6,10},{7,11},{8,4},{9... | collective-permute-start | bytes 393224 | tf_op jit(solution)/shard_map/ppermute | solution.py:383
  21.9 1.6 %shard_map.54.curvature_ref = f32[8,8,32,256]{3,2,1,0:T(8,128)S(1)} custom-call(f32[8,8,32,256]{3,2,1,0:T(8,128)} %curvature_hbm.1), custom_call_target="tpu_custom_call" | custom-call | bytes 4194304 | tf_op jit(solution)/shard_map/pallas_call | solution.py:355
  23.6 0.0 copy-done
  23.6 2.4 %shard_map.55 = (f32[8,8,32,256]{3,2,1,0:T(8,128)S(1)}, f32[8,128]{1,0:T(8,128)S(1)}) custom-call(f32[8,8,32,256]{3,2,1,0:T(8,128)S(1)} %copy-done, f32[8,8,32,256]{3,2,1,0:T(8,128)S(1)} %shard_map.54.curvature_ref), custom_call_target="tpu_custom_call" | custom-call | flops 14155776 | bytes 6291456 | tf_op jit(solution)/shard_map/pallas_call | solution.py:363
  26.0 0.0 collective-permute-done.4.far_ref
  26.0 0.0 collective-permute-done.6.halo_ref
  26.0 0.4 shard_map.56
  26.4 0.0 collective-permute-done.3.halo_ref
  26.4 0.4 shard_map.57
  26.8 18.7 %all_to_all.5.rows_ref = f32[128,1,128]{2,1,0:T(1,128)S(1)} all-to-all(f32[128,1,128]{2,1,0:T(1,128)S(1)} %get-tuple-element.33), channel_id=1, replica_groups=mesh['cuts_0'=2,'cuts_1'=4,'cuts_2'=4,'event_0'=2,'event_1'=2] {'cuts_0'..., dimensions={0} | all-to-all | bytes 131072 | tf_op jit(solution)/shard_map/all_to_all | solution.py:398
  45.5 1.3 %shard_map.58 = (f32[8,32,256]{2,1,0:T(8,128)}, f32[8,32,256]{2,1,0:T(8,128)}) custom-call(f32[128,1,128]{2,1,0:T(1,128)S(1)} %all_to_all.5.rows_ref, f32[4,32,256]{2,1,0:T(8,128)S(1)} %get-tuple-element.34.far_ref, f32[4,32,256]{2,1,0:T(8,128)S(1)} %get-tuple-element.35.near_ref, f32[8,8,32,256]{3,2,1,0:T(8,128)S(1)} %copy-done, ...), custom_call_target="tpu_custom_call" | custom-call | flops 2228224 | bytes 4718592 | tf_op jit(solution)/shard_map/pallas_call | solution.py:399
  (2 shorter events, 0.0 us)
Async XLA Ops:
  2.4 4.4 %collective-permute-start = (f32[3,4,32,256]{3,2,1,0:T(8,128)S(1)}, f32[3,4,32,256]{3,2,1,0:T(8,128)S(1)}, u32[]{:S(2)}, u32[]{:S(2)}) collective-permute-start(f32[3,4,32,256]{3,2,1,0:T(8,128)S(1)} %get-tuple-element.23), channel_id=1, source_target_pairs={{0,1},{1,0},{2,3},{3,2},{4,5},{5,4},{6,7},{7,6},{8,9},{9,8},{10,11... | collective-permute-start | bytes 1179656 | tf_op jit(solution)/shard_map/ppermute | solution.py:313
  3.9 1.5 %collective-permute-start.1 = (f32[4,32,256]{2,1,0:T(8,128)S(1)}, f32[4,32,256]{2,1,0:T(8,128)S(1)}, u32[]{:S(2)}, u32[]{:S(2)}) collective-permute-start(f32[4,32,256]{2,1,0:T(8,128)S(1)} %get-tuple-element.25), channel_id=1, source_target_pairs={{0,1},{1,0},{2,3},{3,2},{4,5},{5,4},{6,7},{7,6},{8,9},{9,8},{10,11... | collective-permute-start | bytes 393224 | tf_op jit(solution)/shard_map/ppermute | solution.py:313
  5.4 4.8 %collective-permute-start.2 = (f32[4,32,256]{2,1,0:T(8,128)S(1)}, f32[4,32,256]{2,1,0:T(8,128)S(1)}, u32[]{:S(2)}, u32[]{:S(2)}) collective-permute-start(f32[4,32,256]{2,1,0:T(8,128)S(1)} %add.6), channel_id=1, source_target_pairs={{0,2},{2,0},{1,3},{3,1},{4,6},{6,4},{5,7},{7,5},{8,10},{10,8},{9,1... | collective-permute-start | bytes 393224 | tf_op jit(solution)/shard_map/ppermute | solution.py:313
  6.8 6.8 %collective-permute-start.5 = (f32[4,32,256]{2,1,0:T(8,128)S(1)}, f32[4,32,256]{2,1,0:T(8,128)S(1)}, u32[]{:S(2)}, u32[]{:S(2)}) collective-permute-start(f32[4,32,256]{2,1,0:T(8,128)S(1)} %fusion), channel_id=1, source_target_pairs={{0,2},{2,0},{1,3},{3,1},{4,6},{6,4},{5,7},{7,5},{8,10},{10,8},{9,1... | collective-permute-start | bytes 393224 | tf_op jit(solution)/shard_map/ppermute | solution.py:313
  10.4 15.6 %collective-permute-start.4 = (f32[4,32,256]{2,1,0:T(8,128)S(1)}, f32[4,32,256]{2,1,0:T(8,128)S(1)}, u32[]{:S(2)}, u32[]{:S(2)}) collective-permute-start(f32[4,32,256]{2,1,0:T(8,128)S(1)} %shard_map.52), channel_id=1, source_target_pairs={{0,2},{1,3},{2,0},{3,1},{4,4},{5,5},{6,6},{7,7},{8,8},{9,9},{10,10... | collective-permute-start | bytes 393224 | tf_op jit(solution)/shard_map/ppermute | solution.py:384
  13.9 9.7 %copy-start = (f32[8,8,32,256]{3,2,1,0:T(8,128)S(1)}, f32[8,8,32,256]{3,2,1,0:T(8,128)}, u32[]{:S(2)}) copy-start(f32[8,8,32,256]{3,2,1,0:T(8,128)} %steps_ref.7) | copy-start | bytes 6291460
  13.9 12.1 %collective-permute-start.6 = (f32[4,32,256]{2,1,0:T(8,128)S(1)}, f32[4,32,256]{2,1,0:T(8,128)S(1)}, u32[]{:S(2)}, u32[]{:S(2)}) collective-permute-start(f32[4,32,256]{2,1,0:T(8,128)S(1)} %shard_map.53.near_ref), channel_id=1, source_target_pairs={{0,4},{4,0},{8,12},{12,8},{16,20},{20,16},{24,28},{28,24},{32,36},... | collective-permute-start | bytes 393224 | tf_op jit(solution)/shard_map/ppermute | solution.py:386
  15.1 11.3 %collective-permute-start.3 = (f32[4,32,256]{2,1,0:T(8,128)S(1)}, f32[4,32,256]{2,1,0:T(8,128)S(1)}, u32[]{:S(2)}, u32[]{:S(2)}) collective-permute-start(f32[4,32,256]{2,1,0:T(8,128)S(1)} %shard_map.52), channel_id=1, source_target_pairs={{0,126},{1,127},{2,124},{3,125},{4,8},{5,9},{6,10},{7,11},{8,4},{9... | collective-permute-start | bytes 393224 | tf_op jit(solution)/shard_map/ppermute | solution.py:383
where the time goes:
time: 47 us; the launch traced here: 46.8 us
  blocking collectives  18.7 us (40%)
  starting transfers between devices  14.5 us (31%)
  Pallas kernels  8.21 us (17%)
  waiting for transfers between devices  4.57 us (10%)
  between operations  0.74 us (2%)
    all_to_all x1, blocking collectives, shards(): arrived = lax.all_to_all(outgoing, CUTS_EVENT, 0, 0, tiled=True)  18.7 us
    ppermute x1, starting transfers between devices, shards(): far_halo = lax.ppermute(far_plane, CUTS_EVENT, pairs)  6.89 us
    ppermute x4, waiting for transfers between devices, swapped(): return lax.ppermute(x, axis, [(0, 1), (1, 0)])  4.56 us
    ppermute x1, starting transfers between devices, shards(): far_plane = lax.ppermute(far_plane, CUTS_EVENT, returns)  3.23 us
    ppermute x4, starting transfers between devices, swapped(): return lax.ppermute(x, axis, [(0, 1), (1, 0)])  3.18 us
    pallas_call x1, Pallas kernels, shards(): call(gram_kernel, [(steps.shape, jnp.float32), row], 2 * 108 * size, 12 *...  2.41 us
    pallas_call x1, Pallas kernels, shards(): call(fetch_kernel, [(curvature.shape, jnp.float32)], 0, 8 * curvature.siz...  1.6 us
    pallas_call x1, Pallas kernels, shards(): call(far_radial_kernel, [half] * 4 + [((RIM, rad_len, lats), jnp.float32)...  1.39 us
  transfers between devices with their start and end apart: 7, of which 2 were waited for; matrix products, arithmetic and copies ran while one was open for 0% of the time, Pallas kernels for 10%

commit v1 on v0

--- a/solution.py
+++ b/solution.py
@@ -87,9 +87,7 @@
         )
         return jnp.concatenate([jnp.concatenate([m, m], axis=1) for m in split(matrix)], axis=0)
 
-    cut = cut_number()
-    at_wrap = jnp.logical_or(cut == 0, cut == lax.axis_size(CUTS) - 1)
-    weights = weights_of(jnp.where(at_wrap, part ^ 2, part))
+    weights = weights_of(jnp.where(cut_number() == 0, part ^ 2, part))
     weights_ref[...] = weights_of(part)
     copies[0].wait()
     radial_products(far_ref, weights, keep_ref, pass_ref, send_keep_ref, send_pass_ref)
@@ -372,16 +370,16 @@
         return call(kernel, [half], 4 * lats * size, 8 * size)(*parts, high, low)[0]
 
     far_plane = plane_of(2, far_keep, rest, far_chip)
-    pairs, returns = [], []
+    pairs = []
     for c in range(cuts):
-        other, flip = (((c - 1) ^ 1) + 1) % cuts, 0
-        if c in (0, cuts - 1):
-            other, flip = cuts - 1 - c, 2
-        for e in range(events):
-            pairs.append((c * events + e, other * events + (e ^ flip)))
-            returns.append((c * events + e, c * events + (e ^ flip)))
+        other, flip = (((c - 1) ^ 1) + 1) % cuts if c else cuts - 1, 2 if c == 0 else 0
+        pairs += [(c * events + e, other * events + (e ^ flip)) for e in range(events)]
     far_halo = lax.ppermute(far_plane, CUTS_EVENT, pairs)
-    far_plane = lax.ppermute(far_plane, CUTS_EVENT, returns)
+    far_plane = lax.ppermute(
+        far_plane,
+        CUTS_EVENT,
+        [(e, e ^ 2) for e in range(events)] + [(d, d) for d in range(events, cuts * events)],
+    )
     near_plane = plane_of(1, near_keep, rest, near_chip)
     near_halo = lax.ppermute(near_plane, CUTS, [(c, c ^ 1) for c in range(cuts)])
     padded = [pltpu.VMEM((3, RIM, rows, lats), jnp.float32)]

time: 47 us -> 46.3 us (0.985)
  blocking collectives: 18.7 us -> 18 us
    all_to_all x1, blocking collectives: 18.7 us -> 18 us  [shards(): arrived = lax.all_to_all(outgoing, CUTS_EVENT, 0, 0, tiled=True)]
where the time goes in v1:
time: 46.3 us; the launch traced here: 46.1 us
  blocking collectives  18 us (39%)
  starting transfers between devices  14.5 us (31%)
  Pallas kernels  8.21 us (18%)
  waiting for transfers between devices  4.57 us (10%)
  between operations  0.74 us (2%)
    all_to_all x1, blocking collectives, shards(): arrived = lax.all_to_all(outgoing, CUTS_EVENT, 0, 0, tiled=True)  18 us
    ppermute x1, starting transfers between devices, shards(): far_halo = lax.ppermute(far_plane, CUTS_EVENT, pairs)  6.89 us
    ppermute x4, waiting for transfers between devices, swapped(): return lax.ppermute(x, axis, [(0, 1), (1, 0)])  4.56 us
    ppermute x1, starting transfers between devices, shards(): lax.ppermute(far_plane, CUTS_EVENT, [(e, e ^ 2) for e in range(events)] +...  3.23 us
    ppermute x4, starting transfers between devices, swapped(): return lax.ppermute(x, axis, [(0, 1), (1, 0)])  3.18 us
    pallas_call x1, Pallas kernels, shards(): call(gram_kernel, [(steps.shape, jnp.float32), row], 2 * 108 * size, 12 *...  2.41 us
    pallas_call x1, Pallas kernels, shards(): call(fetch_kernel, [(curvature.shape, jnp.float32)], 0, 8 * curvature.siz...  1.6 us
    pallas_call x1, Pallas kernels, shards(): call(far_radial_kernel, [half] * 4 + [((RIM, rad_len, lats), jnp.float32)...  1.39 us
  transfers between devices with their start and end apart: 7, of which 2 were waited for; matrix products, arithmetic and copies ran while one was open for 0% of the time, Pallas kernels for 10%

profile of v1, /device:TPU:1, one launch (start us, length us, event | category | flops | bytes accessed | tf_op | source)
XLA Modules:
  0.0 46.1 jit_solution(4395605271024401865)
XLA Ops:
  0.6 1.4 %shard_map.50 = (f32[4,32,256]{2,1,0:T(8,128)S(1)}, f32[4,32,256]{2,1,0:T(8,128)S(1)}, f32[4,32,256]{2,1,0:T(8,128)S(1)}, f32[4,32,256]{2,1,0:T(8,128)S(1)}, f32...) custom-call(f32[1,8,128,256]{3,2,1,0:T(8,128)} %kernels_ref.1), custom_call_target="tpu_custom_call" | custom-call | flops 134217728 | bytes 2097152 | tf_op jit(solution)/shard_map/pallas_call | solution.py:330
  2.0 0.4 shard_map.51
  2.4 1.5 %collective-permute-start = (f32[3,4,32,256]{3,2,1,0:T(8,128)S(1)}, f32[3,4,32,256]{3,2,1,0:T(8,128)S(1)}, u32[]{:S(2)}, u32[]{:S(2)}) collective-permute-start(f32[3,4,32,256]{3,2,1,0:T(8,128)S(1)} %get-tuple-element.23), channel_id=1, source_target_pairs={{0,1},{1,0},{2,3},{3,2},{4,5},{5,4},{6,7},{7,6},{8,9},{9,8},{10,11... | collective-permute-start | bytes 1179656 | tf_op jit(solution)/shard_map/ppermute | solution.py:311
  3.8 0.1 collective-permute-start.1
  3.9 1.4 %collective-permute-done.1 = f32[4,32,256]{2,1,0:T(8,128)S(1)} collective-permute-done((f32[4,32,256]{2,1,0:T(8,128)S(1)}, f32[4,32,256]{2,1,0:T(8,128)S(1)}, u32[]{:S(2)}, u32[]{:S(2)}) %collective-permute-start.1) | collective-permute-done | bytes 131104 | tf_op jit(solution)/shard_map/ppermute | solution.py:311
  5.4 1.4 %collective-permute-start.2 = (f32[4,32,256]{2,1,0:T(8,128)S(1)}, f32[4,32,256]{2,1,0:T(8,128)S(1)}, u32[]{:S(2)}, u32[]{:S(2)}) collective-permute-start(f32[4,32,256]{2,1,0:T(8,128)S(1)} %add.6), channel_id=1, source_target_pairs={{0,2},{2,0},{1,3},{3,1},{4,6},{6,4},{5,7},{7,5},{8,10},{10,8},{9,1... | collective-permute-start | bytes 393224 | tf_op jit(solution)/shard_map/ppermute | solution.py:311
  6.8 0.0 collective-permute-done.rest_ref
  6.8 0.2 collective-permute-start.5
  7.1 3.1 %collective-permute-done.2.chip_ref = f32[4,32,256]{2,1,0:T(8,128)S(1)} collective-permute-done((f32[4,32,256]{2,1,0:T(8,128)S(1)}, f32[4,32,256]{2,1,0:T(8,128)S(1)}, u32[]{:S(2)}, u32[]{:S(2)}) %collective-permute-start.2) | collective-permute-done | bytes 131104 | tf_op jit(solution)/shard_map/ppermute | solution.py:311
  10.2 0.2 shard_map.52
  10.4 3.2 %collective-permute-start.4 = (f32[4,32,256]{2,1,0:T(8,128)S(1)}, f32[4,32,256]{2,1,0:T(8,128)S(1)}, u32[]{:S(2)}, u32[]{:S(2)}) collective-permute-start(f32[4,32,256]{2,1,0:T(8,128)S(1)} %shard_map.52), channel_id=1, source_target_pairs={{0,2},{1,3},{2,0},{3,1},{4,4},{5,5},{6,6},{7,7},{8,8},{9,9},{10,10... | collective-permute-start | bytes 393224 | tf_op jit(solution)/shard_map/ppermute | solution.py:378
  13.6 0.0 collective-permute-done.5.chip_ref
  13.7 0.2 shard_map.53.near_ref
  13.9 0.0 copy-start
  13.9 1.2 %collective-permute-start.6 = (f32[4,32,256]{2,1,0:T(8,128)S(1)}, f32[4,32,256]{2,1,0:T(8,128)S(1)}, u32[]{:S(2)}, u32[]{:S(2)}) collective-permute-start(f32[4,32,256]{2,1,0:T(8,128)S(1)} %shard_map.53.near_ref), channel_id=1, source_target_pairs={{0,4},{4,0},{8,12},{12,8},{16,20},{20,16},{24,28},{28,24},{32,36},... | collective-permute-start | bytes 393224 | tf_op jit(solution)/shard_map/ppermute | solution.py:384
  15.1 6.9 %collective-permute-start.3 = (f32[4,32,256]{2,1,0:T(8,128)S(1)}, f32[4,32,256]{2,1,0:T(8,128)S(1)}, u32[]{:S(2)}, u32[]{:S(2)}) collective-permute-start(f32[4,32,256]{2,1,0:T(8,128)S(1)} %shard_map.52), channel_id=1, source_target_pairs={{0,126},{1,127},{2,124},{3,125},{4,8},{5,9},{6,10},{7,11},{8,4},{9... | collective-permute-start | bytes 393224 | tf_op jit(solution)/shard_map/ppermute | solution.py:377
  21.9 1.6 %shard_map.54.curvature_ref = f32[8,8,32,256]{3,2,1,0:T(8,128)S(1)} custom-call(f32[8,8,32,256]{3,2,1,0:T(8,128)} %curvature_hbm.1), custom_call_target="tpu_custom_call" | custom-call | bytes 4194304 | tf_op jit(solution)/shard_map/pallas_call | solution.py:353
  23.6 0.0 copy-done
  23.6 2.4 %shard_map.55 = (f32[8,8,32,256]{3,2,1,0:T(8,128)S(1)}, f32[8,128]{1,0:T(8,128)S(1)}) custom-call(f32[8,8,32,256]{3,2,1,0:T(8,128)S(1)} %copy-done, f32[8,8,32,256]{3,2,1,0:T(8,128)S(1)} %shard_map.54.curvature_ref), custom_call_target="tpu_custom_call" | custom-call | flops 14155776 | bytes 6291456 | tf_op jit(solution)/shard_map/pallas_call | solution.py:361
  26.0 0.0 collective-permute-done.4.far_ref
  26.0 0.0 collective-permute-done.6.halo_ref
  26.0 0.4 shard_map.56
  26.4 0.0 collective-permute-done.3.halo_ref
  26.4 0.4 shard_map.57
  26.8 18.0 %all_to_all.5.rows_ref = f32[128,1,128]{2,1,0:T(1,128)S(1)} all-to-all(f32[128,1,128]{2,1,0:T(1,128)S(1)} %get-tuple-element.33), channel_id=1, replica_groups=mesh['cuts_0'=2,'cuts_1'=4,'cuts_2'=4,'event_0'=2,'event_1'=2] {'cuts_0'..., dimensions={0} | all-to-all | bytes 131072 | tf_op jit(solution)/shard_map/all_to_all | solution.py:396
  44.8 1.3 %shard_map.58 = (f32[8,32,256]{2,1,0:T(8,128)}, f32[8,32,256]{2,1,0:T(8,128)}) custom-call(f32[128,1,128]{2,1,0:T(1,128)S(1)} %all_to_all.5.rows_ref, f32[4,32,256]{2,1,0:T(8,128)S(1)} %get-tuple-element.34.far_ref, f32[4,32,256]{2,1,0:T(8,128)S(1)} %get-tuple-element.35.near_ref, f32[8,8,32,256]{3,2,1,0:T(8,128)S(1)} %copy-done, ...), custom_call_target="tpu_custom_call" | custom-call | flops 2228224 | bytes 4718592 | tf_op jit(solution)/shard_map/pallas_call | solution.py:397
  (2 shorter events, 0.0 us)
Async XLA Ops:
  2.4 4.4 %collective-permute-start = (f32[3,4,32,256]{3,2,1,0:T(8,128)S(1)}, f32[3,4,32,256]{3,2,1,0:T(8,128)S(1)}, u32[]{:S(2)}, u32[]{:S(2)}) collective-permute-start(f32[3,4,32,256]{3,2,1,0:T(8,128)S(1)} %get-tuple-element.23), channel_id=1, source_target_pairs={{0,1},{1,0},{2,3},{3,2},{4,5},{5,4},{6,7},{7,6},{8,9},{9,8},{10,11... | collective-permute-start | bytes 1179656 | tf_op jit(solution)/shard_map/ppermute | solution.py:311
  3.8 1.5 %collective-permute-start.1 = (f32[4,32,256]{2,1,0:T(8,128)S(1)}, f32[4,32,256]{2,1,0:T(8,128)S(1)}, u32[]{:S(2)}, u32[]{:S(2)}) collective-permute-start(f32[4,32,256]{2,1,0:T(8,128)S(1)} %get-tuple-element.25), channel_id=1, source_target_pairs={{0,1},{1,0},{2,3},{3,2},{4,5},{5,4},{6,7},{7,6},{8,9},{9,8},{10,11... | collective-permute-start | bytes 393224 | tf_op jit(solution)/shard_map/ppermute | solution.py:311
  5.4 4.8 %collective-permute-start.2 = (f32[4,32,256]{2,1,0:T(8,128)S(1)}, f32[4,32,256]{2,1,0:T(8,128)S(1)}, u32[]{:S(2)}, u32[]{:S(2)}) collective-permute-start(f32[4,32,256]{2,1,0:T(8,128)S(1)} %add.6), channel_id=1, source_target_pairs={{0,2},{2,0},{1,3},{3,1},{4,6},{6,4},{5,7},{7,5},{8,10},{10,8},{9,1... | collective-permute-start | bytes 393224 | tf_op jit(solution)/shard_map/ppermute | solution.py:311
  6.8 6.8 %collective-permute-start.5 = (f32[4,32,256]{2,1,0:T(8,128)S(1)}, f32[4,32,256]{2,1,0:T(8,128)S(1)}, u32[]{:S(2)}, u32[]{:S(2)}) collective-permute-start(f32[4,32,256]{2,1,0:T(8,128)S(1)} %fusion), channel_id=1, source_target_pairs={{0,2},{2,0},{1,3},{3,1},{4,6},{6,4},{5,7},{7,5},{8,10},{10,8},{9,1... | collective-permute-start | bytes 393224 | tf_op jit(solution)/shard_map/ppermute | solution.py:311
  10.4 15.6 %collective-permute-start.4 = (f32[4,32,256]{2,1,0:T(8,128)S(1)}, f32[4,32,256]{2,1,0:T(8,128)S(1)}, u32[]{:S(2)}, u32[]{:S(2)}) collective-permute-start(f32[4,32,256]{2,1,0:T(8,128)S(1)} %shard_map.52), channel_id=1, source_target_pairs={{0,2},{1,3},{2,0},{3,1},{4,4},{5,5},{6,6},{7,7},{8,8},{9,9},{10,10... | collective-permute-start | bytes 393224 | tf_op jit(solution)/shard_map/ppermute | solution.py:378
  13.9 9.7 %copy-start = (f32[8,8,32,256]{3,2,1,0:T(8,128)S(1)}, f32[8,8,32,256]{3,2,1,0:T(8,128)}, u32[]{:S(2)}) copy-start(f32[8,8,32,256]{3,2,1,0:T(8,128)} %steps_ref.7) | copy-start | bytes 6291460
  13.9 12.1 %collective-permute-start.6 = (f32[4,32,256]{2,1,0:T(8,128)S(1)}, f32[4,32,256]{2,1,0:T(8,128)S(1)}, u32[]{:S(2)}, u32[]{:S(2)}) collective-permute-start(f32[4,32,256]{2,1,0:T(8,128)S(1)} %shard_map.53.near_ref), channel_id=1, source_target_pairs={{0,4},{4,0},{8,12},{12,8},{16,20},{20,16},{24,28},{28,24},{32,36},... | collective-permute-start | bytes 393224 | tf_op jit(solution)/shard_map/ppermute | solution.py:384
  15.1 11.3 %collective-permute-start.3 = (f32[4,32,256]{2,1,0:T(8,128)S(1)}, f32[4,32,256]{2,1,0:T(8,128)S(1)}, u32[]{:S(2)}, u32[]{:S(2)}) collective-permute-start(f32[4,32,256]{2,1,0:T(8,128)S(1)} %shard_map.52), channel_id=1, source_target_pairs={{0,126},{1,127},{2,124},{3,125},{4,8},{5,9},{6,10},{7,11},{8,4},{9... | collective-permute-start | bytes 393224 | tf_op jit(solution)/shard_map/ppermute | solution.py:377

commit v2 on v1

--- a/solution.py
+++ b/solution.py
@@ -151,18 +151,26 @@
     return lax.fori_loop(0, lons, step, [jnp.zeros((8, LANES), jnp.float32)] * size)
 
 
-def fetch_kernel(curvature_hbm, curvature_ref, semaphore):
-    copy = pltpu.make_async_copy(curvature_hbm, curvature_ref, semaphore)
-    copy.start()
-    copy.wait()
-
-
-def gram_kernel(steps_ref, curvature_ref, changes_ref, row_ref):
+def first_gram_kernel(
+    steps_hbm, curvature_hbm, steps_ref, changes_ref, row_ref, curvature_ref, semaphores
+):
     lons, *plane = steps_ref.shape[1:]
+
+    def fetches(a):
+        pairs = ((steps_hbm, steps_ref), (curvature_hbm, curvature_ref))
+        return [
+            pltpu.make_async_copy(source.at[:, a], target.at[:, a], semaphores.at[k, a])
+            for k, (source, target) in enumerate(pairs)
+        ]
+
+    for a in range(lons):
+        for fetch in fetches(a):
+            fetch.start()
     half = PAIRS // 2
-    upper = [(i, j) for i in range(PAIRS) for j in range(i, PAIRS)]
-
-    def first(a, sums):
+
+    def step(a, sums):
+        for fetch in fetches(a):
+            fetch.wait()
         for at in spots(plane):
             steps = [steps_ref[(i, a, *at)] for i in range(half)]
             changes = [None] * PAIRS
@@ -173,7 +181,15 @@
             sums = [sums[k] + steps[k // PAIRS] * changes[k % PAIRS] for k in range(half * PAIRS)]
         return sums
 
-    def second(a, sums):
+    row_ref[...] = placed(enumerate(summed_over(lons, step, half * PAIRS)))
+
+
+def second_gram_kernel(steps_ref, changes_ref, first_ref, row_ref):
+    lons, *plane = steps_ref.shape[1:]
+    half = PAIRS // 2
+    upper = [(i, j) for i in range(PAIRS) for j in range(i, PAIRS)]
+
+    def mixed(a, sums):
         for at in spots(plane):
             steps = [steps_ref[(i, a, *at)] for i in range(half, PAIRS)]
             changes = [changes_ref[(i, a, *at)] for i in range(PAIRS)]
@@ -186,8 +202,7 @@
             sums = [value + changes[i] * changes[j] for value, (i, j) in zip(sums, upper)]
         return sums
 
-    row = placed(enumerate(summed_over(lons, first, half * PAIRS)))
-    row = row + placed(enumerate(summed_over(lons, second, half * PAIRS), half * PAIRS))
+    row = first_ref[...] + placed(enumerate(summed_over(lons, mixed, half * PAIRS), half * PAIRS))
     row_ref[...] = row + placed(enumerate(summed_over(lons, squares, len(upper)), SQUARES))
 
 
@@ -350,20 +365,20 @@
     rest = swapped(rest, "event_1")
     near_chip = swapped(near_pass + rest[0], "event_0")
     row = ((8, LANES), jnp.float32)
-    (held_curvature,) = call(
-        fetch_kernel,
-        [(curvature.shape, jnp.float32)],
-        0,
-        8 * curvature.size,
-        in_specs=[pl.BlockSpec(memory_space=pltpu.HBM)],
-        scratch_shapes=[pltpu.SemaphoreType.DMA],
-    )(in_hbm(curvature))
-    changes, gram = call(
-        gram_kernel,
-        [(steps.shape, jnp.float32), row],
-        2 * 108 * size,
-        12 * steps.size,
-    )(steps, held_curvature)
+    held_steps, changes, first_row = call(
+        first_gram_kernel,
+        [(steps.shape, jnp.float32)] * 2 + [row],
+        2 * 40 * size,
+        16 * steps.size,
+        in_specs=[pl.BlockSpec(memory_space=pltpu.HBM)] * 2,
+        scratch_shapes=[
+            pltpu.VMEM(curvature.shape, jnp.float32),
+            pltpu.SemaphoreType.DMA((2, lons)),
+        ],
+    )(in_hbm(steps), in_hbm(curvature))
+    (gram,) = call(second_gram_kernel, [row], 2 * 68 * size, 8 * steps.size)(
+        held_steps, changes, first_row
+    )
 
     def plane_of(slot, *parts):
         kernel = functools.partial(latitude_kernel, slot)
@@ -385,14 +400,14 @@
     padded = [pltpu.VMEM((3, RIM, rows, lats), jnp.float32)]
     near_gradient, near_row = call(
         near_product_kernel, [half, row], 2 * 20 * size, 4 * 10 * size, scratch_shapes=padded
-    )(near_halo, near_plane, far_plane, steps, changes, gram)
+    )(near_halo, near_plane, far_plane, held_steps, changes, gram)
     far_gradient, outgoing = call(
         far_product_kernel,
         [half, ((cuts * events, 1, LANES), jnp.float32)],
         2 * 20 * size,
         4 * 10 * size,
         scratch_shapes=padded,
-    )(far_halo, far_plane, near_plane, steps, changes, near_row)
+    )(far_halo, far_plane, near_plane, held_steps, changes, near_row)
     arrived = lax.all_to_all(outgoing, CUTS_EVENT, 0, 0, tiled=True)
     return call(
         direction_kernel,
@@ -401,7 +416,7 @@
         4 * 18 * size,
         out_specs=[pl.BlockSpec(memory_space=pltpu.HBM)] * 2,
         scratch_shapes=[pltpu.VMEM((lons, rows, lats), jnp.float32), pltpu.SemaphoreType.DMA((6,))],
-    )(arrived, far_gradient, near_gradient, steps, changes)
+    )(arrived, far_gradient, near_gradient, held_steps, changes)
 
 
 def solution(mesh):

time: 46.3 us -> 46.3 us (level)
  transfers between devices with their start and end apart: 7 -> 7, of which waited for: 2 -> 2; matrix products, arithmetic and copies ran while one was open for 0% -> 0% of each run, Pallas kernels for 10% -> 11%
where the time goes in v2:
time: 46.3 us; the launch traced here: 46.1 us
  blocking collectives  18 us (39%)
  starting transfers between devices  14.5 us (31%)
  Pallas kernels  8.27 us (18%)
  waiting for transfers between devices  4.57 us (10%)
  between operations  0.72 us (2%)
    all_to_all x1, blocking collectives, shards(): arrived = lax.all_to_all(outgoing, CUTS_EVENT, 0, 0, tiled=True)  18 us
    ppermute x1, starting transfers between devices, shards(): far_halo = lax.ppermute(far_plane, CUTS_EVENT, pairs)  6.89 us
    ppermute x4, waiting for transfers between devices, swapped(): return lax.ppermute(x, axis, [(0, 1), (1, 0)])  4.56 us
    ppermute x1, starting transfers between devices, shards(): lax.ppermute(far_plane, CUTS_EVENT, [(e, e ^ 2) for e in range(events)] +...  3.23 us
    ppermute x4, starting transfers between devices, swapped(): return lax.ppermute(x, axis, [(0, 1), (1, 0)])  3.18 us
    pallas_call x1, Pallas kernels, shards(): call(first_gram_kernel, [(steps.shape, jnp.float32)] * 2 + [row], 2 * 40...  2.48 us
    pallas_call x1, Pallas kernels, shards(): call(second_gram_kernel, [row], 2 * 68 * size, 8 * steps.size)  1.55 us
    pallas_call x1, Pallas kernels, shards(): call(far_radial_kernel, [half] * 4 + [((RIM, rad_len, lats), jnp.float32)...  1.39 us
  transfers between devices with their start and end apart: 7, of which 2 were waited for; matrix products, arithmetic and copies ran while one was open for 0% of the time, Pallas kernels for 11%

profile of v2, /device:TPU:1, one launch (start us, length us, event | category | flops | bytes accessed | tf_op | source)
XLA Modules:
  0.0 46.1 jit_solution(3701249028942641831)
XLA Ops:
  0.6 1.4 %shard_map.50 = (f32[4,32,256]{2,1,0:T(8,128)S(1)}, f32[4,32,256]{2,1,0:T(8,128)S(1)}, f32[4,32,256]{2,1,0:T(8,128)S(1)}, f32[4,32,256]{2,1,0:T(8,128)S(1)}, f32...) custom-call(f32[1,8,128,256]{3,2,1,0:T(8,128)} %kernels_ref.1), custom_call_target="tpu_custom_call" | custom-call | flops 134217728 | bytes 2097152 | tf_op jit(solution)/shard_map/pallas_call | solution.py:345
  2.0 0.4 shard_map.51
  2.4 1.5 %collective-permute-start = (f32[3,4,32,256]{3,2,1,0:T(8,128)S(1)}, f32[3,4,32,256]{3,2,1,0:T(8,128)S(1)}, u32[]{:S(2)}, u32[]{:S(2)}) collective-permute-start(f32[3,4,32,256]{3,2,1,0:T(8,128)S(1)} %get-tuple-element.24), channel_id=1, source_target_pairs={{0,1},{1,0},{2,3},{3,2},{4,5},{5,4},{6,7},{7,6},{8,9},{9,8},{10,11... | collective-permute-start | bytes 1179656 | tf_op jit(solution)/shard_map/ppermute | solution.py:326
  3.8 0.1 collective-permute-start.1
  3.9 1.4 %collective-permute-done.1 = f32[4,32,256]{2,1,0:T(8,128)S(1)} collective-permute-done((f32[4,32,256]{2,1,0:T(8,128)S(1)}, f32[4,32,256]{2,1,0:T(8,128)S(1)}, u32[]{:S(2)}, u32[]{:S(2)}) %collective-permute-start.1) | collective-permute-done | bytes 131104 | tf_op jit(solution)/shard_map/ppermute | solution.py:326
  5.4 1.4 %collective-permute-start.2 = (f32[4,32,256]{2,1,0:T(8,128)S(1)}, f32[4,32,256]{2,1,0:T(8,128)S(1)}, u32[]{:S(2)}, u32[]{:S(2)}) collective-permute-start(f32[4,32,256]{2,1,0:T(8,128)S(1)} %add.6), channel_id=1, source_target_pairs={{0,2},{2,0},{1,3},{3,1},{4,6},{6,4},{5,7},{7,5},{8,10},{10,8},{9,1... | collective-permute-start | bytes 393224 | tf_op jit(solution)/shard_map/ppermute | solution.py:326
  6.8 0.0 collective-permute-done.rest_ref
  6.8 0.2 collective-permute-start.5
  7.1 3.1 %collective-permute-done.2.chip_ref = f32[4,32,256]{2,1,0:T(8,128)S(1)} collective-permute-done((f32[4,32,256]{2,1,0:T(8,128)S(1)}, f32[4,32,256]{2,1,0:T(8,128)S(1)}, u32[]{:S(2)}, u32[]{:S(2)}) %collective-permute-start.2) | collective-permute-done | bytes 131104 | tf_op jit(solution)/shard_map/ppermute | solution.py:326
  10.2 0.2 shard_map.52
  10.4 3.2 %collective-permute-start.4 = (f32[4,32,256]{2,1,0:T(8,128)S(1)}, f32[4,32,256]{2,1,0:T(8,128)S(1)}, u32[]{:S(2)}, u32[]{:S(2)}) collective-permute-start(f32[4,32,256]{2,1,0:T(8,128)S(1)} %shard_map.52), channel_id=1, source_target_pairs={{0,2},{1,3},{2,0},{3,1},{4,4},{5,5},{6,6},{7,7},{8,8},{9,9},{10,10... | collective-permute-start | bytes 393224 | tf_op jit(solution)/shard_map/ppermute | solution.py:393
  13.6 0.0 collective-permute-done.5.chip_ref
  13.7 0.2 shard_map.53.near_ref
  13.9 1.2 %collective-permute-start.6 = (f32[4,32,256]{2,1,0:T(8,128)S(1)}, f32[4,32,256]{2,1,0:T(8,128)S(1)}, u32[]{:S(2)}, u32[]{:S(2)}) collective-permute-start(f32[4,32,256]{2,1,0:T(8,128)S(1)} %shard_map.53.near_ref), channel_id=1, source_target_pairs={{0,4},{4,0},{8,12},{12,8},{16,20},{20,16},{24,28},{28,24},{32,36},... | collective-permute-start | bytes 393224 | tf_op jit(solution)/shard_map/ppermute | solution.py:399
  15.0 6.9 %collective-permute-start.3 = (f32[4,32,256]{2,1,0:T(8,128)S(1)}, f32[4,32,256]{2,1,0:T(8,128)S(1)}, u32[]{:S(2)}, u32[]{:S(2)}) collective-permute-start(f32[4,32,256]{2,1,0:T(8,128)S(1)} %shard_map.52), channel_id=1, source_target_pairs={{0,126},{1,127},{2,124},{3,125},{4,8},{5,9},{6,10},{7,11},{8,4},{9... | collective-permute-start | bytes 393224 | tf_op jit(solution)/shard_map/ppermute | solution.py:392
  21.9 2.5 %shard_map.54 = (f32[8,8,32,256]{3,2,1,0:T(8,128)S(1)}, f32[8,8,32,256]{3,2,1,0:T(8,128)S(1)}, f32[8,128]{1,0:T(8,128)S(1)}) custom-call(f32[8,8,32,256]{3,2,1,0:T(8,128)} %steps_hbm.1, f32[8,8,32,256]{3,2,1,0:T(8,128)} %curvature_hbm.1), custom_call_target="tpu_custom_call" | custom-call | flops 5242880 | bytes 8388608 | tf_op jit(solution)/shard_map/pallas_call | solution.py:368
  24.4 1.6 %shard_map.55.gram_ref = f32[8,128]{1,0:T(8,128)S(1)} custom-call(f32[8,8,32,256]{3,2,1,0:T(8,128)S(1)} %get-tuple-element.31.steps_ref, f32[8,8,32,256]{3,2,1,0:T(8,128)S(1)} %get-tuple-element.32.changes_ref, f32[8,128]{1,0:T(8,128)S(1)} %get-tuple-element.33.first_ref), custom_call_target="tpu_custom_call" | custom-call | flops 8912896 | bytes 4194304 | tf_op jit(solution)/shard_map/pallas_call | solution.py:379
  26.0 0.0 collective-permute-done.4.far_ref
  26.0 0.0 collective-permute-done.6.halo_ref
  26.0 0.4 shard_map.56
  26.4 0.0 collective-permute-done.3.halo_ref
  26.4 0.4 shard_map.57
  26.8 18.0 %all_to_all.5.rows_ref = f32[128,1,128]{2,1,0:T(1,128)S(1)} all-to-all(f32[128,1,128]{2,1,0:T(1,128)S(1)} %get-tuple-element.35), channel_id=1, replica_groups=mesh['cuts_0'=2,'cuts_1'=4,'cuts_2'=4,'event_0'=2,'event_1'=2] {'cuts_0'..., dimensions={0} | all-to-all | bytes 131072 | tf_op jit(solution)/shard_map/all_to_all | solution.py:411
  44.8 1.3 %shard_map.58 = (f32[8,32,256]{2,1,0:T(8,128)}, f32[8,32,256]{2,1,0:T(8,128)}) custom-call(f32[128,1,128]{2,1,0:T(1,128)S(1)} %all_to_all.5.rows_ref, f32[4,32,256]{2,1,0:T(8,128)S(1)} %get-tuple-element.36.far_ref, f32[4,32,256]{2,1,0:T(8,128)S(1)} %get-tuple-element.37.near_ref, f32[8,8,32,256]{3,2,1,0:T(8,128)S(1)} %get-tuple-element.31.steps_ref, ...), custom_call_target="tpu_custom_call" | custom-call | flops 2228224 | bytes 4718592 | tf_op jit(solution)/shard_map/pallas_call | solution.py:412
  (2 shorter events, 0.0 us)
Async XLA Ops:
  2.4 4.4 %collective-permute-start = (f32[3,4,32,256]{3,2,1,0:T(8,128)S(1)}, f32[3,4,32,256]{3,2,1,0:T(8,128)S(1)}, u32[]{:S(2)}, u32[]{:S(2)}) collective-permute-start(f32[3,4,32,256]{3,2,1,0:T(8,128)S(1)} %get-tuple-element.24), channel_id=1, source_target_pairs={{0,1},{1,0},{2,3},{3,2},{4,5},{5,4},{6,7},{7,6},{8,9},{9,8},{10,11... | collective-permute-start | bytes 1179656 | tf_op jit(solution)/shard_map/ppermute | solution.py:326
  3.8 1.5 %collective-permute-start.1 = (f32[4,32,256]{2,1,0:T(8,128)S(1)}, f32[4,32,256]{2,1,0:T(8,128)S(1)}, u32[]{:S(2)}, u32[]{:S(2)}) collective-permute-start(f32[4,32,256]{2,1,0:T(8,128)S(1)} %get-tuple-element.26), channel_id=1, source_target_pairs={{0,1},{1,0},{2,3},{3,2},{4,5},{5,4},{6,7},{7,6},{8,9},{9,8},{10,11... | collective-permute-start | bytes 393224 | tf_op jit(solution)/shard_map/ppermute | solution.py:326
  5.4 4.8 %collective-permute-start.2 = (f32[4,32,256]{2,1,0:T(8,128)S(1)}, f32[4,32,256]{2,1,0:T(8,128)S(1)}, u32[]{:S(2)}, u32[]{:S(2)}) collective-permute-start(f32[4,32,256]{2,1,0:T(8,128)S(1)} %add.6), channel_id=1, source_target_pairs={{0,2},{2,0},{1,3},{3,1},{4,6},{6,4},{5,7},{7,5},{8,10},{10,8},{9,1... | collective-permute-start | bytes 393224 | tf_op jit(solution)/shard_map/ppermute | solution.py:326
  6.8 6.8 %collective-permute-start.5 = (f32[4,32,256]{2,1,0:T(8,128)S(1)}, f32[4,32,256]{2,1,0:T(8,128)S(1)}, u32[]{:S(2)}, u32[]{:S(2)}) collective-permute-start(f32[4,32,256]{2,1,0:T(8,128)S(1)} %fusion), channel_id=1, source_target_pairs={{0,2},{2,0},{1,3},{3,1},{4,6},{6,4},{5,7},{7,5},{8,10},{10,8},{9,1... | collective-permute-start | bytes 393224 | tf_op jit(solution)/shard_map/ppermute | solution.py:326
  10.4 15.6 %collective-permute-start.4 = (f32[4,32,256]{2,1,0:T(8,128)S(1)}, f32[4,32,256]{2,1,0:T(8,128)S(1)}, u32[]{:S(2)}, u32[]{:S(2)}) collective-permute-start(f32[4,32,256]{2,1,0:T(8,128)S(1)} %shard_map.52), channel_id=1, source_target_pairs={{0,2},{1,3},{2,0},{3,1},{4,4},{5,5},{6,6},{7,7},{8,8},{9,9},{10,10... | collective-permute-start | bytes 393224 | tf_op jit(solution)/shard_map/ppermute | solution.py:393
  13.9 12.1 %collective-permute-start.6 = (f32[4,32,256]{2,1,0:T(8,128)S(1)}, f32[4,32,256]{2,1,0:T(8,128)S(1)}, u32[]{:S(2)}, u32[]{:S(2)}) collective-permute-start(f32[4,32,256]{2,1,0:T(8,128)S(1)} %shard_map.53.near_ref), channel_id=1, source_target_pairs={{0,4},{4,0},{8,12},{12,8},{16,20},{20,16},{24,28},{28,24},{32,36},... | collective-permute-start | bytes 393224 | tf_op jit(solution)/shard_map/ppermute | solution.py:399
  15.0 11.3 %collective-permute-start.3 = (f32[4,32,256]{2,1,0:T(8,128)S(1)}, f32[4,32,256]{2,1,0:T(8,128)S(1)}, u32[]{:S(2)}, u32[]{:S(2)}) collective-permute-start(f32[4,32,256]{2,1,0:T(8,128)S(1)} %shard_map.52), channel_id=1, source_target_pairs={{0,126},{1,127},{2,124},{3,125},{4,8},{5,9},{6,10},{7,11},{8,4},{9... | collective-permute-start | bytes 393224 | tf_op jit(solution)/shard_map/ppermute | solution.py:392

commit v3 on v1

--- a/solution.py
+++ b/solution.py
@@ -243,7 +243,8 @@
     ]
     for copy in written:
         copy.start()
-    row = jnp.broadcast_to(jnp.sum(rows_ref[...], axis=0), (8, LANES))
+    row = jnp.sum(jnp.sum(rows_ref[...], axis=0), axis=0, keepdims=True)
+    row = jnp.broadcast_to(row, (8, LANES))
     lanes = lane_numbers()
     pairs = lax.broadcasted_iota(jnp.int32, (8, LANES), 0)
 
@@ -388,12 +389,13 @@
     )(near_halo, near_plane, far_plane, steps, changes, gram)
     far_gradient, outgoing = call(
         far_product_kernel,
-        [half, ((cuts * events, 1, LANES), jnp.float32)],
+        [half, ((cuts * events // 8, 8, LANES), jnp.float32)],
         2 * 20 * size,
         4 * 10 * size,
         scratch_shapes=padded,
     )(far_halo, far_plane, near_plane, steps, changes, near_row)
-    arrived = lax.all_to_all(outgoing, CUTS_EVENT, 0, 0, tiled=True)
+    outgoing = outgoing.reshape(cuts * events, 1, LANES)
+    arrived = lax.all_to_all(outgoing, CUTS_EVENT, 0, 0, tiled=True).reshape(-1, 8, LANES)
     return call(
         direction_kernel,
         [block] * 2,

time: 46.3 us -> 46.1 us (level)
  no operation moved by 1% of the time
where the time goes in v3:
time: 46.1 us; the launch traced here: 45.9 us
  blocking collectives  18 us (39%)
  starting transfers between devices  14.5 us (31%)
  Pallas kernels  8.07 us (18%)
  waiting for transfers between devices  4.57 us (10%)
  between operations  0.74 us (2%)
    all_to_all x1, blocking collectives, shards(): lax.all_to_all(outgoing, CUTS_EVENT, 0, 0, tiled=True).reshape(-1, 8, LANES)  18 us
    ppermute x1, starting transfers between devices, shards(): far_halo = lax.ppermute(far_plane, CUTS_EVENT, pairs)  6.89 us
    ppermute x4, waiting for transfers between devices, swapped(): return lax.ppermute(x, axis, [(0, 1), (1, 0)])  4.56 us
    ppermute x1, starting transfers between devices, shards(): lax.ppermute(far_plane, CUTS_EVENT, [(e, e ^ 2) for e in range(events)] +...  3.23 us
    ppermute x4, starting transfers between devices, swapped(): return lax.ppermute(x, axis, [(0, 1), (1, 0)])  3.18 us
    pallas_call x1, Pallas kernels, shards(): call(gram_kernel, [(steps.shape, jnp.float32), row], 2 * 108 * size, 12 *...  2.41 us
    pallas_call x1, Pallas kernels, shards(): call(fetch_kernel, [(curvature.shape, jnp.float32)], 0, 8 * curvature.siz...  1.6 us
    pallas_call x1, Pallas kernels, shards(): call(far_radial_kernel, [half] * 4 + [((RIM, rad_len, lats), jnp.float32)...  1.39 us
  transfers between devices with their start and end apart: 7, of which 2 were waited for; matrix products, arithmetic and copies ran while one was open for 0% of the time, Pallas kernels for 10%

profile of v3, /device:TPU:1, one launch (start us, length us, event | category | flops | bytes accessed | tf_op | source)
XLA Modules:
  0.0 45.9 jit_solution(15380947935150852441)
XLA Ops:
  0.6 1.4 %shard_map.50 = (f32[4,32,256]{2,1,0:T(8,128)S(1)}, f32[4,32,256]{2,1,0:T(8,128)S(1)}, f32[4,32,256]{2,1,0:T(8,128)S(1)}, f32[4,32,256]{2,1,0:T(8,128)S(1)}, f32...) custom-call(f32[1,8,128,256]{3,2,1,0:T(8,128)} %kernels_ref.1), custom_call_target="tpu_custom_call" | custom-call | flops 134217728 | bytes 2097152 | tf_op jit(solution)/shard_map/pallas_call | solution.py:331
  2.0 0.4 shard_map.51
  2.4 1.5 %collective-permute-start = (f32[3,4,32,256]{3,2,1,0:T(8,128)S(1)}, f32[3,4,32,256]{3,2,1,0:T(8,128)S(1)}, u32[]{:S(2)}, u32[]{:S(2)}) collective-permute-start(f32[3,4,32,256]{3,2,1,0:T(8,128)S(1)} %get-tuple-element.23), channel_id=1, source_target_pairs={{0,1},{1,0},{2,3},{3,2},{4,5},{5,4},{6,7},{7,6},{8,9},{9,8},{10,11... | collective-permute-start | bytes 1179656 | tf_op jit(solution)/shard_map/ppermute | solution.py:312
  3.8 0.1 collective-permute-start.1
  3.9 1.4 %collective-permute-done.1 = f32[4,32,256]{2,1,0:T(8,128)S(1)} collective-permute-done((f32[4,32,256]{2,1,0:T(8,128)S(1)}, f32[4,32,256]{2,1,0:T(8,128)S(1)}, u32[]{:S(2)}, u32[]{:S(2)}) %collective-permute-start.1) | collective-permute-done | bytes 131104 | tf_op jit(solution)/shard_map/ppermute | solution.py:312
  5.4 1.4 %collective-permute-start.2 = (f32[4,32,256]{2,1,0:T(8,128)S(1)}, f32[4,32,256]{2,1,0:T(8,128)S(1)}, u32[]{:S(2)}, u32[]{:S(2)}) collective-permute-start(f32[4,32,256]{2,1,0:T(8,128)S(1)} %add.6), channel_id=1, source_target_pairs={{0,2},{2,0},{1,3},{3,1},{4,6},{6,4},{5,7},{7,5},{8,10},{10,8},{9,1... | collective-permute-start | bytes 393224 | tf_op jit(solution)/shard_map/ppermute | solution.py:312
  6.8 0.0 collective-permute-done.rest_ref
  6.8 0.2 collective-permute-start.5
  7.1 3.1 %collective-permute-done.2.chip_ref = f32[4,32,256]{2,1,0:T(8,128)S(1)} collective-permute-done((f32[4,32,256]{2,1,0:T(8,128)S(1)}, f32[4,32,256]{2,1,0:T(8,128)S(1)}, u32[]{:S(2)}, u32[]{:S(2)}) %collective-permute-start.2) | collective-permute-done | bytes 131104 | tf_op jit(solution)/shard_map/ppermute | solution.py:312
  10.2 0.2 shard_map.52
  10.4 3.2 %collective-permute-start.4 = (f32[4,32,256]{2,1,0:T(8,128)S(1)}, f32[4,32,256]{2,1,0:T(8,128)S(1)}, u32[]{:S(2)}, u32[]{:S(2)}) collective-permute-start(f32[4,32,256]{2,1,0:T(8,128)S(1)} %shard_map.52), channel_id=1, source_target_pairs={{0,2},{1,3},{2,0},{3,1},{4,4},{5,5},{6,6},{7,7},{8,8},{9,9},{10,10... | collective-permute-start | bytes 393224 | tf_op jit(solution)/shard_map/ppermute | solution.py:379
  13.6 0.0 collective-permute-done.5.chip_ref
  13.7 0.2 shard_map.53.near_ref
  13.9 0.0 copy-start
  13.9 1.2 %collective-permute-start.6 = (f32[4,32,256]{2,1,0:T(8,128)S(1)}, f32[4,32,256]{2,1,0:T(8,128)S(1)}, u32[]{:S(2)}, u32[]{:S(2)}) collective-permute-start(f32[4,32,256]{2,1,0:T(8,128)S(1)} %shard_map.53.near_ref), channel_id=1, source_target_pairs={{0,4},{4,0},{8,12},{12,8},{16,20},{20,16},{24,28},{28,24},{32,36},... | collective-permute-start | bytes 393224 | tf_op jit(solution)/shard_map/ppermute | solution.py:385
  15.1 6.9 %collective-permute-start.3 = (f32[4,32,256]{2,1,0:T(8,128)S(1)}, f32[4,32,256]{2,1,0:T(8,128)S(1)}, u32[]{:S(2)}, u32[]{:S(2)}) collective-permute-start(f32[4,32,256]{2,1,0:T(8,128)S(1)} %shard_map.52), channel_id=1, source_target_pairs={{0,126},{1,127},{2,124},{3,125},{4,8},{5,9},{6,10},{7,11},{8,4},{9... | collective-permute-start | bytes 393224 | tf_op jit(solution)/shard_map/ppermute | solution.py:378
  21.9 1.6 %shard_map.54.curvature_ref = f32[8,8,32,256]{3,2,1,0:T(8,128)S(1)} custom-call(f32[8,8,32,256]{3,2,1,0:T(8,128)} %curvature_hbm.1), custom_call_target="tpu_custom_call" | custom-call | bytes 4194304 | tf_op jit(solution)/shard_map/pallas_call | solution.py:354
  23.6 0.0 copy-done
  23.6 2.4 %shard_map.55 = (f32[8,8,32,256]{3,2,1,0:T(8,128)S(1)}, f32[8,128]{1,0:T(8,128)S(1)}) custom-call(f32[8,8,32,256]{3,2,1,0:T(8,128)S(1)} %copy-done, f32[8,8,32,256]{3,2,1,0:T(8,128)S(1)} %shard_map.54.curvature_ref), custom_call_target="tpu_custom_call" | custom-call | flops 14155776 | bytes 6291456 | tf_op jit(solution)/shard_map/pallas_call | solution.py:362
  26.0 0.0 collective-permute-done.4.far_ref
  26.0 0.0 collective-permute-done.6.halo_ref
  26.0 0.4 shard_map.56
  26.4 0.0 collective-permute-done.3.halo_ref
  26.4 0.4 shard_map.57
  26.7 18.0 %all_to_all.5 = f32[128,1,128]{2,1,0:T(1,128)S(1)} all-to-all(f32[128,1,128]{2,1,0:T(1,128)S(1)} %bitcast.9), channel_id=1, replica_groups=mesh['cuts_0'=2,'cuts_1'=4,'cuts_2'=4,'event_0'=2,'event_1'=2] {'cuts_0'..., dimensions={0} | all-to-all | bytes 131072 | tf_op jit(solution)/shard_map/all_to_all | solution.py:398
  44.8 1.1 %shard_map.58 = (f32[8,32,256]{2,1,0:T(8,128)}, f32[8,32,256]{2,1,0:T(8,128)}) custom-call(f32[16,8,128]{2,1,0:T(8,128)S(1)} %bitcast.8, f32[4,32,256]{2,1,0:T(8,128)S(1)} %get-tuple-element.34.far_ref, f32[4,32,256]{2,1,0:T(8,128)S(1)} %get-tuple-element.35.near_ref, f32[8,8,32,256]{3,2,1,0:T(8,128)S(1)} %copy-done, ...), custom_call_target="tpu_custom_call" | custom-call | flops 2228224 | bytes 4718592 | tf_op jit(solution)/shard_map/pallas_call | solution.py:399
  (2 shorter events, 0.0 us)
Async XLA Ops:
  2.4 4.4 %collective-permute-start = (f32[3,4,32,256]{3,2,1,0:T(8,128)S(1)}, f32[3,4,32,256]{3,2,1,0:T(8,128)S(1)}, u32[]{:S(2)}, u32[]{:S(2)}) collective-permute-start(f32[3,4,32,256]{3,2,1,0:T(8,128)S(1)} %get-tuple-element.23), channel_id=1, source_target_pairs={{0,1},{1,0},{2,3},{3,2},{4,5},{5,4},{6,7},{7,6},{8,9},{9,8},{10,11... | collective-permute-start | bytes 1179656 | tf_op jit(solution)/shard_map/ppermute | solution.py:312
  3.8 1.5 %collective-permute-start.1 = (f32[4,32,256]{2,1,0:T(8,128)S(1)}, f32[4,32,256]{2,1,0:T(8,128)S(1)}, u32[]{:S(2)}, u32[]{:S(2)}) collective-permute-start(f32[4,32,256]{2,1,0:T(8,128)S(1)} %get-tuple-element.25), channel_id=1, source_target_pairs={{0,1},{1,0},{2,3},{3,2},{4,5},{5,4},{6,7},{7,6},{8,9},{9,8},{10,11... | collective-permute-start | bytes 393224 | tf_op jit(solution)/shard_map/ppermute | solution.py:312
  5.4 4.8 %collective-permute-start.2 = (f32[4,32,256]{2,1,0:T(8,128)S(1)}, f32[4,32,256]{2,1,0:T(8,128)S(1)}, u32[]{:S(2)}, u32[]{:S(2)}) collective-permute-start(f32[4,32,256]{2,1,0:T(8,128)S(1)} %add.6), channel_id=1, source_target_pairs={{0,2},{2,0},{1,3},{3,1},{4,6},{6,4},{5,7},{7,5},{8,10},{10,8},{9,1... | collective-permute-start | bytes 393224 | tf_op jit(solution)/shard_map/ppermute | solution.py:312
  6.8 6.8 %collective-permute-start.5 = (f32[4,32,256]{2,1,0:T(8,128)S(1)}, f32[4,32,256]{2,1,0:T(8,128)S(1)}, u32[]{:S(2)}, u32[]{:S(2)}) collective-permute-start(f32[4,32,256]{2,1,0:T(8,128)S(1)} %fusion), channel_id=1, source_target_pairs={{0,2},{2,0},{1,3},{3,1},{4,6},{6,4},{5,7},{7,5},{8,10},{10,8},{9,1... | collective-permute-start | bytes 393224 | tf_op jit(solution)/shard_map/ppermute | solution.py:312
  10.4 15.6 %collective-permute-start.4 = (f32[4,32,256]{2,1,0:T(8,128)S(1)}, f32[4,32,256]{2,1,0:T(8,128)S(1)}, u32[]{:S(2)}, u32[]{:S(2)}) collective-permute-start(f32[4,32,256]{2,1,0:T(8,128)S(1)} %shard_map.52), channel_id=1, source_target_pairs={{0,2},{1,3},{2,0},{3,1},{4,4},{5,5},{6,6},{7,7},{8,8},{9,9},{10,10... | collective-permute-start | bytes 393224 | tf_op jit(solution)/shard_map/ppermute | solution.py:379
  13.9 9.7 %copy-start = (f32[8,8,32,256]{3,2,1,0:T(8,128)S(1)}, f32[8,8,32,256]{3,2,1,0:T(8,128)}, u32[]{:S(2)}) copy-start(f32[8,8,32,256]{3,2,1,0:T(8,128)} %steps_ref.7) | copy-start | bytes 6291460
  13.9 12.1 %collective-permute-start.6 = (f32[4,32,256]{2,1,0:T(8,128)S(1)}, f32[4,32,256]{2,1,0:T(8,128)S(1)}, u32[]{:S(2)}, u32[]{:S(2)}) collective-permute-start(f32[4,32,256]{2,1,0:T(8,128)S(1)} %shard_map.53.near_ref), channel_id=1, source_target_pairs={{0,4},{4,0},{8,12},{12,8},{16,20},{20,16},{24,28},{28,24},{32,36},... | collective-permute-start | bytes 393224 | tf_op jit(solution)/shard_map/ppermute | solution.py:385
  15.1 11.3 %collective-permute-start.3 = (f32[4,32,256]{2,1,0:T(8,128)S(1)}, f32[4,32,256]{2,1,0:T(8,128)S(1)}, u32[]{:S(2)}, u32[]{:S(2)}) collective-permute-start(f32[4,32,256]{2,1,0:T(8,128)S(1)} %shard_map.52), channel_id=1, source_target_pairs={{0,126},{1,127},{2,124},{3,125},{4,8},{5,9},{6,10},{7,11},{8,4},{9... | collective-permute-start | bytes 393224 | tf_op jit(solution)/shard_map/ppermute | solution.py:378

commit v4 on v2

--- a/solution.py
+++ b/solution.py
@@ -258,7 +258,8 @@
     ]
     for copy in written:
         copy.start()
-    row = jnp.broadcast_to(jnp.sum(rows_ref[...], axis=0), (8, LANES))
+    row = jnp.sum(jnp.sum(rows_ref[...], axis=0), axis=0, keepdims=True)
+    row = jnp.broadcast_to(row, (8, LANES))
     lanes = lane_numbers()
     pairs = lax.broadcasted_iota(jnp.int32, (8, LANES), 0)
 
@@ -403,12 +404,13 @@
     )(near_halo, near_plane, far_plane, held_steps, changes, gram)
     far_gradient, outgoing = call(
         far_product_kernel,
-        [half, ((cuts * events, 1, LANES), jnp.float32)],
+        [half, ((cuts * events // 8, 8, LANES), jnp.float32)],
         2 * 20 * size,
         4 * 10 * size,
         scratch_shapes=padded,
     )(far_halo, far_plane, near_plane, held_steps, changes, near_row)
-    arrived = lax.all_to_all(outgoing, CUTS_EVENT, 0, 0, tiled=True)
+    outgoing = outgoing.reshape(cuts * events, 1, LANES)
+    arrived = lax.all_to_all(outgoing, CUTS_EVENT, 0, 0, tiled=True).reshape(-1, 8, LANES)
     return call(
         direction_kernel,
         [block] * 2,

time: 46.3 us -> 46.1 us (level)
  no operation moved by 1% of the time
where the time goes in v4:
time: 46.1 us; the launch traced here: 45.9 us
  blocking collectives  18 us (39%)
  starting transfers between devices  14.5 us (31%)
  Pallas kernels  8.12 us (18%)
  waiting for transfers between devices  4.57 us (10%)
  between operations  0.72 us (2%)
    all_to_all x1, blocking collectives, shards(): lax.all_to_all(outgoing, CUTS_EVENT, 0, 0, tiled=True).reshape(-1, 8, LANES)  18 us
    ppermute x1, starting transfers between devices, shards(): far_halo = lax.ppermute(far_plane, CUTS_EVENT, pairs)  6.89 us
    ppermute x4, waiting for transfers between devices, swapped(): return lax.ppermute(x, axis, [(0, 1), (1, 0)])  4.56 us
    ppermute x1, starting transfers between devices, shards(): lax.ppermute(far_plane, CUTS_EVENT, [(e, e ^ 2) for e in range(events)] +...  3.23 us
    ppermute x4, starting transfers between devices, swapped(): return lax.ppermute(x, axis, [(0, 1), (1, 0)])  3.18 us
    pallas_call x1, Pallas kernels, shards(): call(first_gram_kernel, [(steps.shape, jnp.float32)] * 2 + [row], 2 * 40...  2.48 us
    pallas_call x1, Pallas kernels, shards(): call(second_gram_kernel, [row], 2 * 68 * size, 8 * steps.size)  1.55 us
    pallas_call x1, Pallas kernels, shards(): call(far_radial_kernel, [half] * 4 + [((RIM, rad_len, lats), jnp.float32)...  1.39 us
  transfers between devices with their start and end apart: 7, of which 2 were waited for; matrix products, arithmetic and copies ran while one was open for 0% of the time, Pallas kernels for 11%

profile of v4, /device:TPU:1, one launch (start us, length us, event | category | flops | bytes accessed | tf_op | source)
XLA Modules:
  0.0 45.9 jit_solution(16476039209942392562)
XLA Ops:
  0.6 1.4 %shard_map.50 = (f32[4,32,256]{2,1,0:T(8,128)S(1)}, f32[4,32,256]{2,1,0:T(8,128)S(1)}, f32[4,32,256]{2,1,0:T(8,128)S(1)}, f32[4,32,256]{2,1,0:T(8,128)S(1)}, f32...) custom-call(f32[1,8,128,256]{3,2,1,0:T(8,128)} %kernels_ref.1), custom_call_target="tpu_custom_call" | custom-call | flops 134217728 | bytes 2097152 | tf_op jit(solution)/shard_map/pallas_call | solution.py:346
  2.0 0.4 shard_map.51
  2.4 1.5 %collective-permute-start = (f32[3,4,32,256]{3,2,1,0:T(8,128)S(1)}, f32[3,4,32,256]{3,2,1,0:T(8,128)S(1)}, u32[]{:S(2)}, u32[]{:S(2)}) collective-permute-start(f32[3,4,32,256]{3,2,1,0:T(8,128)S(1)} %get-tuple-element.24), channel_id=1, source_target_pairs={{0,1},{1,0},{2,3},{3,2},{4,5},{5,4},{6,7},{7,6},{8,9},{9,8},{10,11... | collective-permute-start | bytes 1179656 | tf_op jit(solution)/shard_map/ppermute | solution.py:327
  3.8 0.1 collective-permute-start.1
  3.9 1.4 %collective-permute-done.1 = f32[4,32,256]{2,1,0:T(8,128)S(1)} collective-permute-done((f32[4,32,256]{2,1,0:T(8,128)S(1)}, f32[4,32,256]{2,1,0:T(8,128)S(1)}, u32[]{:S(2)}, u32[]{:S(2)}) %collective-permute-start.1) | collective-permute-done | bytes 131104 | tf_op jit(solution)/shard_map/ppermute | solution.py:327
  5.4 1.4 %collective-permute-start.2 = (f32[4,32,256]{2,1,0:T(8,128)S(1)}, f32[4,32,256]{2,1,0:T(8,128)S(1)}, u32[]{:S(2)}, u32[]{:S(2)}) collective-permute-start(f32[4,32,256]{2,1,0:T(8,128)S(1)} %add.6), channel_id=1, source_target_pairs={{0,2},{2,0},{1,3},{3,1},{4,6},{6,4},{5,7},{7,5},{8,10},{10,8},{9,1... | collective-permute-start | bytes 393224 | tf_op jit(solution)/shard_map/ppermute | solution.py:327
  6.8 0.0 collective-permute-done.rest_ref
  6.8 0.2 collective-permute-start.5
  7.1 3.1 %collective-permute-done.2.chip_ref = f32[4,32,256]{2,1,0:T(8,128)S(1)} collective-permute-done((f32[4,32,256]{2,1,0:T(8,128)S(1)}, f32[4,32,256]{2,1,0:T(8,128)S(1)}, u32[]{:S(2)}, u32[]{:S(2)}) %collective-permute-start.2) | collective-permute-done | bytes 131104 | tf_op jit(solution)/shard_map/ppermute | solution.py:327
  10.2 0.2 shard_map.52
  10.4 3.2 %collective-permute-start.4 = (f32[4,32,256]{2,1,0:T(8,128)S(1)}, f32[4,32,256]{2,1,0:T(8,128)S(1)}, u32[]{:S(2)}, u32[]{:S(2)}) collective-permute-start(f32[4,32,256]{2,1,0:T(8,128)S(1)} %shard_map.52), channel_id=1, source_target_pairs={{0,2},{1,3},{2,0},{3,1},{4,4},{5,5},{6,6},{7,7},{8,8},{9,9},{10,10... | collective-permute-start | bytes 393224 | tf_op jit(solution)/shard_map/ppermute | solution.py:394
  13.6 0.0 collective-permute-done.5.chip_ref
  13.7 0.2 shard_map.53.near_ref
  13.9 1.2 %collective-permute-start.6 = (f32[4,32,256]{2,1,0:T(8,128)S(1)}, f32[4,32,256]{2,1,0:T(8,128)S(1)}, u32[]{:S(2)}, u32[]{:S(2)}) collective-permute-start(f32[4,32,256]{2,1,0:T(8,128)S(1)} %shard_map.53.near_ref), channel_id=1, source_target_pairs={{0,4},{4,0},{8,12},{12,8},{16,20},{20,16},{24,28},{28,24},{32,36},... | collective-permute-start | bytes 393224 | tf_op jit(solution)/shard_map/ppermute | solution.py:400
  15.0 6.9 %collective-permute-start.3 = (f32[4,32,256]{2,1,0:T(8,128)S(1)}, f32[4,32,256]{2,1,0:T(8,128)S(1)}, u32[]{:S(2)}, u32[]{:S(2)}) collective-permute-start(f32[4,32,256]{2,1,0:T(8,128)S(1)} %shard_map.52), channel_id=1, source_target_pairs={{0,126},{1,127},{2,124},{3,125},{4,8},{5,9},{6,10},{7,11},{8,4},{9... | collective-permute-start | bytes 393224 | tf_op jit(solution)/shard_map/ppermute | solution.py:393
  21.9 2.5 %shard_map.54 = (f32[8,8,32,256]{3,2,1,0:T(8,128)S(1)}, f32[8,8,32,256]{3,2,1,0:T(8,128)S(1)}, f32[8,128]{1,0:T(8,128)S(1)}) custom-call(f32[8,8,32,256]{3,2,1,0:T(8,128)} %steps_hbm.1, f32[8,8,32,256]{3,2,1,0:T(8,128)} %curvature_hbm.1), custom_call_target="tpu_custom_call" | custom-call | flops 5242880 | bytes 8388608 | tf_op jit(solution)/shard_map/pallas_call | solution.py:369
  24.4 1.6 %shard_map.55.gram_ref = f32[8,128]{1,0:T(8,128)S(1)} custom-call(f32[8,8,32,256]{3,2,1,0:T(8,128)S(1)} %get-tuple-element.31.steps_ref, f32[8,8,32,256]{3,2,1,0:T(8,128)S(1)} %get-tuple-element.32.changes_ref, f32[8,128]{1,0:T(8,128)S(1)} %get-tuple-element.33.first_ref), custom_call_target="tpu_custom_call" | custom-call | flops 8912896 | bytes 4194304 | tf_op jit(solution)/shard_map/pallas_call | solution.py:380
  26.0 0.0 collective-permute-done.4.far_ref
  26.0 0.0 collective-permute-done.6.halo_ref
  26.0 0.4 shard_map.56
  26.4 0.0 collective-permute-done.3.halo_ref
  26.4 0.4 shard_map.57
  26.7 18.0 %all_to_all.5 = f32[128,1,128]{2,1,0:T(1,128)S(1)} all-to-all(f32[128,1,128]{2,1,0:T(1,128)S(1)} %bitcast.9), channel_id=1, replica_groups=mesh['cuts_0'=2,'cuts_1'=4,'cuts_2'=4,'event_0'=2,'event_1'=2] {'cuts_0'..., dimensions={0} | all-to-all | bytes 131072 | tf_op jit(solution)/shard_map/all_to_all | solution.py:413
  44.8 1.2 %shard_map.58 = (f32[8,32,256]{2,1,0:T(8,128)}, f32[8,32,256]{2,1,0:T(8,128)}) custom-call(f32[16,8,128]{2,1,0:T(8,128)S(1)} %bitcast.8, f32[4,32,256]{2,1,0:T(8,128)S(1)} %get-tuple-element.36.far_ref, f32[4,32,256]{2,1,0:T(8,128)S(1)} %get-tuple-element.37.near_ref, f32[8,8,32,256]{3,2,1,0:T(8,128)S(1)} %get-tuple-element.31.steps_ref, ...), custom_call_target="tpu_custom_call" | custom-call | flops 2228224 | bytes 4718592 | tf_op jit(solution)/shard_map/pallas_call | solution.py:414
  (2 shorter events, 0.0 us)
Async XLA Ops:
  2.4 4.4 %collective-permute-start = (f32[3,4,32,256]{3,2,1,0:T(8,128)S(1)}, f32[3,4,32,256]{3,2,1,0:T(8,128)S(1)}, u32[]{:S(2)}, u32[]{:S(2)}) collective-permute-start(f32[3,4,32,256]{3,2,1,0:T(8,128)S(1)} %get-tuple-element.24), channel_id=1, source_target_pairs={{0,1},{1,0},{2,3},{3,2},{4,5},{5,4},{6,7},{7,6},{8,9},{9,8},{10,11... | collective-permute-start | bytes 1179656 | tf_op jit(solution)/shard_map/ppermute | solution.py:327
  3.8 1.5 %collective-permute-start.1 = (f32[4,32,256]{2,1,0:T(8,128)S(1)}, f32[4,32,256]{2,1,0:T(8,128)S(1)}, u32[]{:S(2)}, u32[]{:S(2)}) collective-permute-start(f32[4,32,256]{2,1,0:T(8,128)S(1)} %get-tuple-element.26), channel_id=1, source_target_pairs={{0,1},{1,0},{2,3},{3,2},{4,5},{5,4},{6,7},{7,6},{8,9},{9,8},{10,11... | collective-permute-start | bytes 393224 | tf_op jit(solution)/shard_map/ppermute | solution.py:327
  5.4 4.8 %collective-permute-start.2 = (f32[4,32,256]{2,1,0:T(8,128)S(1)}, f32[4,32,256]{2,1,0:T(8,128)S(1)}, u32[]{:S(2)}, u32[]{:S(2)}) collective-permute-start(f32[4,32,256]{2,1,0:T(8,128)S(1)} %add.6), channel_id=1, source_target_pairs={{0,2},{2,0},{1,3},{3,1},{4,6},{6,4},{5,7},{7,5},{8,10},{10,8},{9,1... | collective-permute-start | bytes 393224 | tf_op jit(solution)/shard_map/ppermute | solution.py:327
  6.8 6.8 %collective-permute-start.5 = (f32[4,32,256]{2,1,0:T(8,128)S(1)}, f32[4,32,256]{2,1,0:T(8,128)S(1)}, u32[]{:S(2)}, u32[]{:S(2)}) collective-permute-start(f32[4,32,256]{2,1,0:T(8,128)S(1)} %fusion), channel_id=1, source_target_pairs={{0,2},{2,0},{1,3},{3,1},{4,6},{6,4},{5,7},{7,5},{8,10},{10,8},{9,1... | collective-permute-start | bytes 393224 | tf_op jit(solution)/shard_map/ppermute | solution.py:327
  10.4 15.6 %collective-permute-start.4 = (f32[4,32,256]{2,1,0:T(8,128)S(1)}, f32[4,32,256]{2,1,0:T(8,128)S(1)}, u32[]{:S(2)}, u32[]{:S(2)}) collective-permute-start(f32[4,32,256]{2,1,0:T(8,128)S(1)} %shard_map.52), channel_id=1, source_target_pairs={{0,2},{1,3},{2,0},{3,1},{4,4},{5,5},{6,6},{7,7},{8,8},{9,9},{10,10... | collective-permute-start | bytes 393224 | tf_op jit(solution)/shard_map/ppermute | solution.py:394
  13.9 12.1 %collective-permute-start.6 = (f32[4,32,256]{2,1,0:T(8,128)S(1)}, f32[4,32,256]{2,1,0:T(8,128)S(1)}, u32[]{:S(2)}, u32[]{:S(2)}) collective-permute-start(f32[4,32,256]{2,1,0:T(8,128)S(1)} %shard_map.53.near_ref), channel_id=1, source_target_pairs={{0,4},{4,0},{8,12},{12,8},{16,20},{20,16},{24,28},{28,24},{32,36},... | collective-permute-start | bytes 393224 | tf_op jit(solution)/shard_map/ppermute | solution.py:400
  15.0 11.3 %collective-permute-start.3 = (f32[4,32,256]{2,1,0:T(8,128)S(1)}, f32[4,32,256]{2,1,0:T(8,128)S(1)}, u32[]{:S(2)}, u32[]{:S(2)}) collective-permute-start(f32[4,32,256]{2,1,0:T(8,128)S(1)} %shard_map.52), channel_id=1, source_target_pairs={{0,126},{1,127},{2,124},{3,125},{4,8},{5,9},{6,10},{7,11},{8,4},{9... | collective-permute-start | bytes 393224 | tf_op jit(solution)/shard_map/ppermute | solution.py:393

commit v5 on v4

--- a/solution.py
+++ b/solution.py
@@ -294,10 +294,10 @@
         changes_part = changes_part + weights[i] * by_step[i]
     change_weights = [scaling * alpha for alpha in alphas]
     copies = []
-    half = RIM // 2
-    for piece in range(4):
-        base, gradient_ref = sides[piece // 2]
-        first = piece % 2 * half
+    half = RIM // 4
+    for piece in range(8):
+        base, gradient_ref = sides[piece // 4]
+        first = piece % 4 * half
         for a, r, b in tiles((half, *far_ref.shape[1:])):
             lon = base + first + a
             value = -(scaling * gradient_ref[first + a, r, b])
@@ -417,7 +417,10 @@
         2 * 17 * size,
         4 * 18 * size,
         out_specs=[pl.BlockSpec(memory_space=pltpu.HBM)] * 2,
-        scratch_shapes=[pltpu.VMEM((lons, rows, lats), jnp.float32), pltpu.SemaphoreType.DMA((6,))],
+        scratch_shapes=[
+            pltpu.VMEM((lons, rows, lats), jnp.float32),
+            pltpu.SemaphoreType.DMA((10,)),
+        ],
     )(arrived, far_gradient, near_gradient, held_steps, changes)
 
 

time: 46.1 us -> 46.1 us (level)
  no operation moved by 1% of the time
where the time goes in v5:
time: 46.1 us; the launch traced here: 45.9 us
  blocking collectives  18 us (39%)
  starting transfers between devices  14.5 us (31%)
  Pallas kernels  8.12 us (18%)
  waiting for transfers between devices  4.57 us (10%)
  between operations  0.72 us (2%)
    all_to_all x1, blocking collectives, shards(): lax.all_to_all(outgoing, CUTS_EVENT, 0, 0, tiled=True).reshape(-1, 8, LANES)  18 us
    ppermute x1, starting transfers between devices, shards(): far_halo = lax.ppermute(far_plane, CUTS_EVENT, pairs)  6.89 us
    ppermute x4, waiting for transfers between devices, swapped(): return lax.ppermute(x, axis, [(0, 1), (1, 0)])  4.56 us
    ppermute x1, starting transfers between devices, shards(): lax.ppermute(far_plane, CUTS_EVENT, [(e, e ^ 2) for e in range(events)] +...  3.23 us
    ppermute x4, starting transfers between devices, swapped(): return lax.ppermute(x, axis, [(0, 1), (1, 0)])  3.18 us
    pallas_call x1, Pallas kernels, shards(): call(first_gram_kernel, [(steps.shape, jnp.float32)] * 2 + [row], 2 * 40...  2.48 us
    pallas_call x1, Pallas kernels, shards(): call(second_gram_kernel, [row], 2 * 68 * size, 8 * steps.size)  1.55 us
    pallas_call x1, Pallas kernels, shards(): call(far_radial_kernel, [half] * 4 + [((RIM, rad_len, lats), jnp.float32)...  1.39 us
  transfers between devices with their start and end apart: 7, of which 2 were waited for; matrix products, arithmetic and copies ran while one was open for 0% of the time, Pallas kernels for 11%

profile of v5, /device:TPU:1, one launch (start us, length us, event | category | flops | bytes accessed | tf_op | source)
XLA Modules:
  0.0 45.9 jit_solution(2218021980022928709)
XLA Ops:
  0.6 1.4 %shard_map.50 = (f32[4,32,256]{2,1,0:T(8,128)S(1)}, f32[4,32,256]{2,1,0:T(8,128)S(1)}, f32[4,32,256]{2,1,0:T(8,128)S(1)}, f32[4,32,256]{2,1,0:T(8,128)S(1)}, f32...) custom-call(f32[1,8,128,256]{3,2,1,0:T(8,128)} %kernels_ref.1), custom_call_target="tpu_custom_call" | custom-call | flops 134217728 | bytes 2097152 | tf_op jit(solution)/shard_map/pallas_call | solution.py:346
  2.0 0.4 shard_map.51
  2.4 1.5 %collective-permute-start = (f32[3,4,32,256]{3,2,1,0:T(8,128)S(1)}, f32[3,4,32,256]{3,2,1,0:T(8,128)S(1)}, u32[]{:S(2)}, u32[]{:S(2)}) collective-permute-start(f32[3,4,32,256]{3,2,1,0:T(8,128)S(1)} %get-tuple-element.24), channel_id=1, source_target_pairs={{0,1},{1,0},{2,3},{3,2},{4,5},{5,4},{6,7},{7,6},{8,9},{9,8},{10,11... | collective-permute-start | bytes 1179656 | tf_op jit(solution)/shard_map/ppermute | solution.py:327
  3.8 0.1 collective-permute-start.1
  3.9 1.4 %collective-permute-done.1 = f32[4,32,256]{2,1,0:T(8,128)S(1)} collective-permute-done((f32[4,32,256]{2,1,0:T(8,128)S(1)}, f32[4,32,256]{2,1,0:T(8,128)S(1)}, u32[]{:S(2)}, u32[]{:S(2)}) %collective-permute-start.1) | collective-permute-done | bytes 131104 | tf_op jit(solution)/shard_map/ppermute | solution.py:327
  5.4 1.4 %collective-permute-start.2 = (f32[4,32,256]{2,1,0:T(8,128)S(1)}, f32[4,32,256]{2,1,0:T(8,128)S(1)}, u32[]{:S(2)}, u32[]{:S(2)}) collective-permute-start(f32[4,32,256]{2,1,0:T(8,128)S(1)} %add.6), channel_id=1, source_target_pairs={{0,2},{2,0},{1,3},{3,1},{4,6},{6,4},{5,7},{7,5},{8,10},{10,8},{9,1... | collective-permute-start | bytes 393224 | tf_op jit(solution)/shard_map/ppermute | solution.py:327
  6.8 0.0 collective-permute-done.rest_ref
  6.8 0.2 collective-permute-start.5
  7.1 3.1 %collective-permute-done.2.chip_ref = f32[4,32,256]{2,1,0:T(8,128)S(1)} collective-permute-done((f32[4,32,256]{2,1,0:T(8,128)S(1)}, f32[4,32,256]{2,1,0:T(8,128)S(1)}, u32[]{:S(2)}, u32[]{:S(2)}) %collective-permute-start.2) | collective-permute-done | bytes 131104 | tf_op jit(solution)/shard_map/ppermute | solution.py:327
  10.2 0.2 shard_map.52
  10.4 3.2 %collective-permute-start.4 = (f32[4,32,256]{2,1,0:T(8,128)S(1)}, f32[4,32,256]{2,1,0:T(8,128)S(1)}, u32[]{:S(2)}, u32[]{:S(2)}) collective-permute-start(f32[4,32,256]{2,1,0:T(8,128)S(1)} %shard_map.52), channel_id=1, source_target_pairs={{0,2},{1,3},{2,0},{3,1},{4,4},{5,5},{6,6},{7,7},{8,8},{9,9},{10,10... | collective-permute-start | bytes 393224 | tf_op jit(solution)/shard_map/ppermute | solution.py:394
  13.6 0.0 collective-permute-done.5.chip_ref
  13.7 0.2 shard_map.53.near_ref
  13.9 1.2 %collective-permute-start.6 = (f32[4,32,256]{2,1,0:T(8,128)S(1)}, f32[4,32,256]{2,1,0:T(8,128)S(1)}, u32[]{:S(2)}, u32[]{:S(2)}) collective-permute-start(f32[4,32,256]{2,1,0:T(8,128)S(1)} %shard_map.53.near_ref), channel_id=1, source_target_pairs={{0,4},{4,0},{8,12},{12,8},{16,20},{20,16},{24,28},{28,24},{32,36},... | collective-permute-start | bytes 393224 | tf_op jit(solution)/shard_map/ppermute | solution.py:400
  15.0 6.9 %collective-permute-start.3 = (f32[4,32,256]{2,1,0:T(8,128)S(1)}, f32[4,32,256]{2,1,0:T(8,128)S(1)}, u32[]{:S(2)}, u32[]{:S(2)}) collective-permute-start(f32[4,32,256]{2,1,0:T(8,128)S(1)} %shard_map.52), channel_id=1, source_target_pairs={{0,126},{1,127},{2,124},{3,125},{4,8},{5,9},{6,10},{7,11},{8,4},{9... | collective-permute-start | bytes 393224 | tf_op jit(solution)/shard_map/ppermute | solution.py:393
  21.9 2.5 %shard_map.54 = (f32[8,8,32,256]{3,2,1,0:T(8,128)S(1)}, f32[8,8,32,256]{3,2,1,0:T(8,128)S(1)}, f32[8,128]{1,0:T(8,128)S(1)}) custom-call(f32[8,8,32,256]{3,2,1,0:T(8,128)} %steps_hbm.1, f32[8,8,32,256]{3,2,1,0:T(8,128)} %curvature_hbm.1), custom_call_target="tpu_custom_call" | custom-call | flops 5242880 | bytes 8388608 | tf_op jit(solution)/shard_map/pallas_call | solution.py:369
  24.4 1.6 %shard_map.55.gram_ref = f32[8,128]{1,0:T(8,128)S(1)} custom-call(f32[8,8,32,256]{3,2,1,0:T(8,128)S(1)} %get-tuple-element.31.steps_ref, f32[8,8,32,256]{3,2,1,0:T(8,128)S(1)} %get-tuple-element.32.changes_ref, f32[8,128]{1,0:T(8,128)S(1)} %get-tuple-element.33.first_ref), custom_call_target="tpu_custom_call" | custom-call | flops 8912896 | bytes 4194304 | tf_op jit(solution)/shard_map/pallas_call | solution.py:380
  26.0 0.0 collective-permute-done.4.far_ref
  26.0 0.0 collective-permute-done.6.halo_ref
  26.0 0.4 shard_map.56
  26.4 0.0 collective-permute-done.3.halo_ref
  26.4 0.4 shard_map.57
  26.7 18.0 %all_to_all.5 = f32[128,1,128]{2,1,0:T(1,128)S(1)} all-to-all(f32[128,1,128]{2,1,0:T(1,128)S(1)} %bitcast.9), channel_id=1, replica_groups=mesh['cuts_0'=2,'cuts_1'=4,'cuts_2'=4,'event_0'=2,'event_1'=2] {'cuts_0'..., dimensions={0} | all-to-all | bytes 131072 | tf_op jit(solution)/shard_map/all_to_all | solution.py:413
  44.8 1.2 %shard_map.58 = (f32[8,32,256]{2,1,0:T(8,128)}, f32[8,32,256]{2,1,0:T(8,128)}) custom-call(f32[16,8,128]{2,1,0:T(8,128)S(1)} %bitcast.8, f32[4,32,256]{2,1,0:T(8,128)S(1)} %get-tuple-element.36.far_ref, f32[4,32,256]{2,1,0:T(8,128)S(1)} %get-tuple-element.37.near_ref, f32[8,8,32,256]{3,2,1,0:T(8,128)S(1)} %get-tuple-element.31.steps_ref, ...), custom_call_target="tpu_custom_call" | custom-call | flops 2228224 | bytes 4718592 | tf_op jit(solution)/shard_map/pallas_call | solution.py:414
  (2 shorter events, 0.0 us)
Async XLA Ops:
  2.4 4.4 %collective-permute-start = (f32[3,4,32,256]{3,2,1,0:T(8,128)S(1)}, f32[3,4,32,256]{3,2,1,0:T(8,128)S(1)}, u32[]{:S(2)}, u32[]{:S(2)}) collective-permute-start(f32[3,4,32,256]{3,2,1,0:T(8,128)S(1)} %get-tuple-element.24), channel_id=1, source_target_pairs={{0,1},{1,0},{2,3},{3,2},{4,5},{5,4},{6,7},{7,6},{8,9},{9,8},{10,11... | collective-permute-start | bytes 1179656 | tf_op jit(solution)/shard_map/ppermute | solution.py:327
  3.8 1.5 %collective-permute-start.1 = (f32[4,32,256]{2,1,0:T(8,128)S(1)}, f32[4,32,256]{2,1,0:T(8,128)S(1)}, u32[]{:S(2)}, u32[]{:S(2)}) collective-permute-start(f32[4,32,256]{2,1,0:T(8,128)S(1)} %get-tuple-element.26), channel_id=1, source_target_pairs={{0,1},{1,0},{2,3},{3,2},{4,5},{5,4},{6,7},{7,6},{8,9},{9,8},{10,11... | collective-permute-start | bytes 393224 | tf_op jit(solution)/shard_map/ppermute | solution.py:327
  5.4 4.8 %collective-permute-start.2 = (f32[4,32,256]{2,1,0:T(8,128)S(1)}, f32[4,32,256]{2,1,0:T(8,128)S(1)}, u32[]{:S(2)}, u32[]{:S(2)}) collective-permute-start(f32[4,32,256]{2,1,0:T(8,128)S(1)} %add.6), channel_id=1, source_target_pairs={{0,2},{2,0},{1,3},{3,1},{4,6},{6,4},{5,7},{7,5},{8,10},{10,8},{9,1... | collective-permute-start | bytes 393224 | tf_op jit(solution)/shard_map/ppermute | solution.py:327
  6.8 6.8 %collective-permute-start.5 = (f32[4,32,256]{2,1,0:T(8,128)S(1)}, f32[4,32,256]{2,1,0:T(8,128)S(1)}, u32[]{:S(2)}, u32[]{:S(2)}) collective-permute-start(f32[4,32,256]{2,1,0:T(8,128)S(1)} %fusion), channel_id=1, source_target_pairs={{0,2},{2,0},{1,3},{3,1},{4,6},{6,4},{5,7},{7,5},{8,10},{10,8},{9,1... | collective-permute-start | bytes 393224 | tf_op jit(solution)/shard_map/ppermute | solution.py:327
  10.4 15.6 %collective-permute-start.4 = (f32[4,32,256]{2,1,0:T(8,128)S(1)}, f32[4,32,256]{2,1,0:T(8,128)S(1)}, u32[]{:S(2)}, u32[]{:S(2)}) collective-permute-start(f32[4,32,256]{2,1,0:T(8,128)S(1)} %shard_map.52), channel_id=1, source_target_pairs={{0,2},{1,3},{2,0},{3,1},{4,4},{5,5},{6,6},{7,7},{8,8},{9,9},{10,10... | collective-permute-start | bytes 393224 | tf_op jit(solution)/shard_map/ppermute | solution.py:394
  13.9 12.1 %collective-permute-start.6 = (f32[4,32,256]{2,1,0:T(8,128)S(1)}, f32[4,32,256]{2,1,0:T(8,128)S(1)}, u32[]{:S(2)}, u32[]{:S(2)}) collective-permute-start(f32[4,32,256]{2,1,0:T(8,128)S(1)} %shard_map.53.near_ref), channel_id=1, source_target_pairs={{0,4},{4,0},{8,12},{12,8},{16,20},{20,16},{24,28},{28,24},{32,36},... | collective-permute-start | bytes 393224 | tf_op jit(solution)/shard_map/ppermute | solution.py:400
  15.0 11.3 %collective-permute-start.3 = (f32[4,32,256]{2,1,0:T(8,128)S(1)}, f32[4,32,256]{2,1,0:T(8,128)S(1)}, u32[]{:S(2)}, u32[]{:S(2)}) collective-permute-start(f32[4,32,256]{2,1,0:T(8,128)S(1)} %shard_map.52), channel_id=1, source_target_pairs={{0,126},{1,127},{2,124},{3,125},{4,8},{5,9},{6,10},{7,11},{8,4},{9... | collective-permute-start | bytes 393224 | tf_op jit(solution)/shard_map/ppermute | solution.py:393
